TPU v7x, 128 devices: a whole 4x4x4 slice. The times are simulated.
128 devices in a mesh: ty: 2 (over core), tx: 64 (over z, y, x).
Axes of the slice: x: 4, y: 4, z: 4, core: 2. Of those that a mesh axis runs over, the one named last changes fastest.
Arguments:
- w_in: float32 [64, 2, 3, 128, 512], P('tx', 'ty')
- w_out: float32 [64, 2, 3, 512, 128], P('tx', 'ty')
- inputs: bfloat16 [64, 2, 7, 2048, 128], P('tx', 'ty')
- targets: bfloat16 [64, 2, 7, 2048, 128], P('tx', 'ty')
Outputs:
- output 1: float32 [64, 2, 3, 128, 512], P('tx', 'ty')
- output 2: float32 [64, 2, 3, 512, 128], P('tx', 'ty')
- output 3: float32 [64, 2, 3, 128, 512], P('tx', 'ty')
- output 4: float32 [64, 2, 3, 512, 128], P('tx', 'ty')
All inputs are finite; a program needn't handle non-finite values.
Results may differ from a plain program's by a relative error of at most 0.00525345.
Values are sent between devices in bfloat16 or wider.
A program may use at most 1 GiB of HBM per device.

v0:
```python
import jax
import jax.numpy as jnp
from jax import lax
from jax.sharding import PartitionSpec as P

EPS = 1e-6
LEARN_RATE = 0.125


def layer_step(hidden, mat_in, mat_out):
    hidden_f32 = hidden.astype(jnp.float32)
    inv_rms = lax.rsqrt(jnp.mean(hidden_f32 * hidden_f32, axis=-1, keepdims=True) + EPS)
    normed = (hidden_f32 * inv_rms).astype(jnp.bfloat16)
    pre_act = jnp.dot(normed, mat_in.astype(jnp.bfloat16), preferred_element_type=jnp.float32)
    gelu_out = jax.nn.gelu(pre_act).astype(jnp.bfloat16)
    mlp_out = jnp.dot(gelu_out, mat_out.astype(jnp.bfloat16), preferred_element_type=jnp.float32)
    return (hidden_f32 + mlp_out).astype(jnp.bfloat16)


def local_loss(w_in, w_out, batch_in, batch_tgt):
    hidden = batch_in
    for layer_idx in range(w_in.shape[0]):
        hidden = layer_step(hidden, w_in[layer_idx], w_out[layer_idx])
    resid_err = hidden.astype(jnp.float32) - batch_tgt.astype(jnp.float32)
    return jnp.mean(resid_err * resid_err)


local_grads = jax.grad(local_loss, argnums=(0, 1))


def neighbour_shift(values, axis_name, axis_size, offset):
    perm_pairs = [(source, (source + offset) % axis_size) for source in range(axis_size)]
    return lax.ppermute(values, axis_name, perm_pairs)


def solution(mesh):
    size_x = mesh.shape['tx']
    size_y = mesh.shape['ty']

    def gossip_mix(values):
        sent_copy = values.astype(jnp.bfloat16)
        from_xm = neighbour_shift(sent_copy, 'tx', size_x, 1)
        from_xp = neighbour_shift(sent_copy, 'tx', size_x, -1)
        from_ym = neighbour_shift(sent_copy, 'ty', size_y, 1)
        from_yp = neighbour_shift(sent_copy, 'ty', size_y, -1)
        summed = values + from_xm.astype(jnp.float32)
        summed = summed + from_xp.astype(jnp.float32)
        summed = summed + from_ym.astype(jnp.float32)
        summed = summed + from_yp.astype(jnp.float32)
        return summed / 5.0

    def device_fn(w_in, w_out, inputs, targets):
        p_in = w_in[0, 0]
        p_out = w_out[0, 0]
        batch_in = inputs[0, 0]
        batch_tgt = targets[0, 0]
        step_size = LEARN_RATE
        grad_in, grad_out = local_grads(p_in, p_out, batch_in[0], batch_tgt[0])
        y_in, y_out = grad_in, grad_out
        for step_idx in range(1, batch_in.shape[0]):
            p_in = gossip_mix(p_in) - step_size * y_in
            p_out = gossip_mix(p_out) - step_size * y_out
            mixed_yin = gossip_mix(y_in)
            mixed_yout = gossip_mix(y_out)
            new_gin, new_gout = local_grads(p_in, p_out, batch_in[step_idx], batch_tgt[step_idx])
            y_in = mixed_yin + new_gin - grad_in
            y_out = mixed_yout + new_gout - grad_out
            grad_in, grad_out = new_gin, new_gout
        return p_in[None, None], p_out[None, None], y_in[None, None], y_out[None, None]

    block_spec = P('tx', 'ty')
    return jax.shard_map(device_fn, mesh=mesh, in_specs=(block_spec, block_spec, block_spec, block_spec), out_specs=(block_spec, block_spec, block_spec, block_spec), check_vma=False)
```

profile of v0, /device:TPU:0, one launch (start us, length us, event | category | flops | bytes accessed | tf_op | source)
XLA Modules:
  0.0 546.8 jit_solution(6630233918633441559)
XLA Ops:
  2.9 8.8 %collective-permute-start.10 = (bf16[3,512,128]{2,1,0:T(8,128)(2,1)}, bf16[3,512,128]{2,1,0:T(8,128)(2,1)}, u32[]{:S(2)}, u32[]{:S(2)}) collective-permute-start(bf16[3,512,128]{2,1,0:T(8,128)(2,1)} %get-tuple-element.53), channel_id=1, source_target_pairs={{0,63},{1,0},{2,1},{3,2},{4,3},{5,4},{6,5},{7,6},{8,7},{9,8},{10,9... | collective-permute-start | bytes 1179656 | tf_op jit(solution)/shard_map/ppermute | solution.py:33
  14.0 7.5 %collective-permute-start.1 = (bf16[3,128,512]{2,1,0:T(8,128)(2,1)}, bf16[3,128,512]{2,1,0:T(8,128)(2,1)}, u32[]{:S(2)}, u32[]{:S(2)}) collective-permute-start(bf16[3,128,512]{2,1,0:T(8,128)(2,1)} %get-tuple-element.55), channel_id=1, source_target_pairs={{0,63},{1,0},{2,1},{3,2},{4,3},{5,4},{6,5},{7,6},{8,7},{9,8},{10,9... | collective-permute-start | bytes 1179656 | tf_op jit(solution)/shard_map/ppermute | solution.py:33
  59.5 6.3 %fusion.462 = bf16[1,128,512]{2,1,0:T(8,128)(2,1)} fusion(f32[2048,512]{1,0:T(8,128)} %get-tuple-element.62, bf16[2048,128]{0,1:T(8,128)(2,1)} %copy-done.83, bf16[1,1,1,2048,128]{3,4,2,1,0:T(8,128)(2,1)S(1)} %copy.36, f32[2048]{0:T(1024)S(1)} %copy-done.189, bf16[1,1,3,512,128]{4,3,2,1,0:T(8,128)(2,1)} %copy-done.123), kind=kOutput, calls=%fused_computation.668 | convolution fusion | flops 559742976 | bytes 5513216 | tf_op jit(solution)/shard_map/transpose(jvp())/dot_general | solution.py:14
  100.6 10.0 %collective-permute-done.9 = bf16[3,512,128]{2,1,0:T(8,128)(2,1)S(1)} collective-permute-done((bf16[3,512,128]{2,1,0:T(8,128)(2,1)}, bf16[3,512,128]{2,1,0:T(8,128)(2,1)S(1)}, u32[]{:S(2)}, u32[]{:S(2)}) %collective-permute-start.9) | collective-permute-done | bytes 393248 | tf_op jit(solution)/shard_map/ppermute | solution.py:33
  134.2 7.4 %collective-permute-start.22 = (bf16[3,512,128]{2,1,0:T(8,128)(2,1)}, bf16[3,512,128]{2,1,0:T(8,128)(2,1)}, u32[]{:S(2)}, u32[]{:S(2)}) collective-permute-start(bf16[3,512,128]{2,1,0:T(8,128)(2,1)} %get-tuple-element.57), channel_id=1, source_target_pairs={{0,63},{1,0},{2,1},{3,2},{4,3},{5,4},{6,5},{7,6},{8,7},{9,8},{10,9... | collective-permute-start | bytes 1179656 | tf_op jit(solution)/shard_map/ppermute | solution.py:33
  141.7 7.5 %collective-permute-start.4 = (bf16[3,128,512]{2,1,0:T(8,128)(2,1)}, bf16[3,128,512]{2,1,0:T(8,128)(2,1)}, u32[]{:S(2)}, u32[]{:S(2)}) collective-permute-start(bf16[3,128,512]{2,1,0:T(8,128)(2,1)} %get-tuple-element.60), channel_id=1, source_target_pairs={{0,63},{1,0},{2,1},{3,2},{4,3},{5,4},{6,5},{7,6},{8,7},{9,8},{10,9... | collective-permute-start | bytes 1179656 | tf_op jit(solution)/shard_map/ppermute | solution.py:33
  151.1 6.2 %fusion.465 = bf16[1,128,512]{2,1,0:T(8,128)(2,1)} fusion(f32[2048,512]{1,0:T(8,128)} %get-tuple-element.72, bf16[2048,128]{0,1:T(8,128)(2,1)S(1)} %fusion.507, bf16[1,1,1,2048,128]{3,4,2,1,0:T(8,128)(2,1)S(1)} %copy-done.58, f32[2048]{0:T(1024)} %copy-done.187, bf16[3,512,128]{2,1,0:T(8,128)(2,1)} %copy-done.121), kind=kOutput, calls=%fused_computation.669 | convolution fusion | flops 559742976 | bytes 5513216 | tf_op jit(solution)/shard_map/transpose(jvp())/dot_general | solution.py:14
  162.0 7.4 %collective-permute-start.7 = (bf16[3,128,512]{2,1,0:T(8,128)(2,1)S(1)}, bf16[3,128,512]{2,1,0:T(8,128)(2,1)S(1)}, u32[]{:S(2)}, u32[]{:S(2)}) collective-permute-start(bf16[3,128,512]{2,1,0:T(8,128)(2,1)S(1)} %copy-done.173), channel_id=1, source_target_pairs={{0,63},{1,0},{2,1},{3,2},{4,3},{5,4},{6,5},{7,6},{8,7},{9,8},{10,9... | collective-permute-start | bytes 1179656 | tf_op jit(solution)/shard_map/ppermute | solution.py:33
  172.7 7.4 %collective-permute-start.19 = (bf16[3,512,128]{2,1,0:T(8,128)(2,1)S(1)}, bf16[3,512,128]{2,1,0:T(8,128)(2,1)S(1)}, u32[]{:S(2)}, u32[]{:S(2)}) collective-permute-start(bf16[3,512,128]{2,1,0:T(8,128)(2,1)S(1)} %copy-done.122), channel_id=1, source_target_pairs={{0,63},{1,0},{2,1},{3,2},{4,3},{5,4},{6,5},{7,6},{8,7},{9,8},{10,9... | collective-permute-start | bytes 1179656 | tf_op jit(solution)/shard_map/ppermute | solution.py:33
  211.3 7.4 %collective-permute-start.34 = (bf16[3,512,128]{2,1,0:T(8,128)(2,1)}, bf16[3,512,128]{2,1,0:T(8,128)(2,1)}, u32[]{:S(2)}, u32[]{:S(2)}) collective-permute-start(bf16[3,512,128]{2,1,0:T(8,128)(2,1)} %get-tuple-element.29), channel_id=1, source_target_pairs={{0,63},{1,0},{2,1},{3,2},{4,3},{5,4},{6,5},{7,6},{8,7},{9,8},{10,9... | collective-permute-start | bytes 1179656 | tf_op jit(solution)/shard_map/ppermute | solution.py:33
  219.5 7.5 %collective-permute-start.16 = (bf16[3,128,512]{2,1,0:T(8,128)(2,1)}, bf16[3,128,512]{2,1,0:T(8,128)(2,1)}, u32[]{:S(2)}, u32[]{:S(2)}) collective-permute-start(bf16[3,128,512]{2,1,0:T(8,128)(2,1)} %convert_element_type.1461), channel_id=1, source_target_pairs={{0,63},{1,0},{2,1},{3,2},{4,3},{5,4},{6,5},{7,6},{8,7},{9,8},{10,9... | collective-permute-start | bytes 1179656 | tf_op jit(solution)/shard_map/ppermute | solution.py:33
  228.9 6.3 %fusion.468 = bf16[1,128,512]{2,1,0:T(8,128)(2,1)} fusion(f32[2048,512]{1,0:T(8,128)} %get-tuple-element.82, bf16[2048,128]{0,1:T(8,128)(2,1)} %fusion.509, bf16[1,1,1,2048,128]{3,4,2,1,0:T(8,128)(2,1)S(1)} %copy-done.55, f32[2048]{0:T(1024)S(1)} %copy-done.186, bf16[3,512,128]{2,1,0:T(8,128)(2,1)} %copy-done.127), kind=kOutput, calls=%fused_computation.670 | convolution fusion | flops 559742976 | bytes 5513216 | tf_op jit(solution)/shard_map/transpose(jvp())/dot_general | solution.py:14
  239.9 7.4 %collective-permute-start.13 = (bf16[3,128,512]{2,1,0:T(8,128)(2,1)S(1)}, bf16[3,128,512]{2,1,0:T(8,128)(2,1)S(1)}, u32[]{:S(2)}, u32[]{:S(2)}) collective-permute-start(bf16[3,128,512]{2,1,0:T(8,128)(2,1)S(1)} %copy-done.74), channel_id=1, source_target_pairs={{0,63},{1,0},{2,1},{3,2},{4,3},{5,4},{6,5},{7,6},{8,7},{9,8},{10,9... | collective-permute-start | bytes 1179656 | tf_op jit(solution)/shard_map/ppermute | solution.py:33
  251.3 7.4 %collective-permute-start.31 = (bf16[3,512,128]{2,1,0:T(8,128)(2,1)S(1)}, bf16[3,512,128]{2,1,0:T(8,128)(2,1)S(1)}, u32[]{:S(2)}, u32[]{:S(2)}) collective-permute-start(bf16[3,512,128]{2,1,0:T(8,128)(2,1)S(1)} %copy-done.128), channel_id=1, source_target_pairs={{0,63},{1,0},{2,1},{3,2},{4,3},{5,4},{6,5},{7,6},{8,7},{9,8},{10,9... | collective-permute-start | bytes 1179656 | tf_op jit(solution)/shard_map/ppermute | solution.py:33
  287.3 7.4 %collective-permute-start.46 = (bf16[3,512,128]{2,1,0:T(8,128)(2,1)}, bf16[3,512,128]{2,1,0:T(8,128)(2,1)}, u32[]{:S(2)}, u32[]{:S(2)}) collective-permute-start(bf16[3,512,128]{2,1,0:T(8,128)(2,1)} %get-tuple-element.22), channel_id=1, source_target_pairs={{0,63},{1,0},{2,1},{3,2},{4,3},{5,4},{6,5},{7,6},{8,7},{9,8},{10,9... | collective-permute-start | bytes 1179656 | tf_op jit(solution)/shard_map/ppermute | solution.py:33
  295.5 7.5 %collective-permute-start.28 = (bf16[3,128,512]{2,1,0:T(8,128)(2,1)}, bf16[3,128,512]{2,1,0:T(8,128)(2,1)}, u32[]{:S(2)}, u32[]{:S(2)}) collective-permute-start(bf16[3,128,512]{2,1,0:T(8,128)(2,1)} %convert_element_type.1522), channel_id=1, source_target_pairs={{0,63},{1,0},{2,1},{3,2},{4,3},{5,4},{6,5},{7,6},{8,7},{9,8},{10,9... | collective-permute-start | bytes 1179656 | tf_op jit(solution)/shard_map/ppermute | solution.py:33
  304.1 6.2 %fusion.471 = bf16[1,128,512]{2,1,0:T(8,128)(2,1)} fusion(f32[2048,512]{1,0:T(8,128)} %get-tuple-element.92, bf16[2048,128]{0,1:T(8,128)(2,1)S(1)} %fusion.511, bf16[1,1,1,2048,128]{3,4,2,1,0:T(8,128)(2,1)S(1)} %copy-done.53, f32[2048]{0:T(1024)} %add_rsqrt_fusion.3, bf16[3,512,128]{2,1,0:T(8,128)(2,1)} %copy-done.129), kind=kOutput, calls=%fused_computation.671 | convolution fusion | flops 559742976 | bytes 5513216 | tf_op jit(solution)/shard_map/transpose(jvp())/dot_general | solution.py:14
  315.0 7.4 %collective-permute-start.25 = (bf16[3,128,512]{2,1,0:T(8,128)(2,1)S(1)}, bf16[3,128,512]{2,1,0:T(8,128)(2,1)S(1)}, u32[]{:S(2)}, u32[]{:S(2)}) collective-permute-start(bf16[3,128,512]{2,1,0:T(8,128)(2,1)S(1)} %copy-done.76), channel_id=1, source_target_pairs={{0,63},{1,0},{2,1},{3,2},{4,3},{5,4},{6,5},{7,6},{8,7},{9,8},{10,9... | collective-permute-start | bytes 1179656 | tf_op jit(solution)/shard_map/ppermute | solution.py:33
  325.7 7.4 %collective-permute-start.43 = (bf16[3,512,128]{2,1,0:T(8,128)(2,1)S(1)}, bf16[3,512,128]{2,1,0:T(8,128)(2,1)S(1)}, u32[]{:S(2)}, u32[]{:S(2)}) collective-permute-start(bf16[3,512,128]{2,1,0:T(8,128)(2,1)S(1)} %copy-done.130), channel_id=1, source_target_pairs={{0,63},{1,0},{2,1},{3,2},{4,3},{5,4},{6,5},{7,6},{8,7},{9,8},{10,9... | collective-permute-start | bytes 1179656 | tf_op jit(solution)/shard_map/ppermute | solution.py:33
  356.9 7.5 %collective-permute-start.40 = (bf16[3,128,512]{2,1,0:T(8,128)(2,1)}, bf16[3,128,512]{2,1,0:T(8,128)(2,1)}, u32[]{:S(2)}, u32[]{:S(2)}) collective-permute-start(bf16[3,128,512]{2,1,0:T(8,128)(2,1)} %convert_element_type.1583), channel_id=1, source_target_pairs={{0,63},{1,0},{2,1},{3,2},{4,3},{5,4},{6,5},{7,6},{8,7},{9,8},{10,9... | collective-permute-start | bytes 1179656 | tf_op jit(solution)/shard_map/ppermute | solution.py:33
  371.2 6.1 %fusion.474 = bf16[1,128,512]{2,1,0:T(8,128)(2,1)} fusion(f32[2048,512]{1,0:T(8,128)} %get-tuple-element.102, bf16[2048,128]{0,1:T(8,128)(2,1)S(1)} %fusion.513, bf16[1,1,1,2048,128]{3,4,2,1,0:T(8,128)(2,1)S(1)} %copy-done.51, f32[2048]{0:T(1024)} %add_rsqrt_fusion.2, bf16[3,512,128]{2,1,0:T(8,128)(2,1)} %copy-done.125), kind=kOutput, calls=%fused_computation.672 | convolution fusion | flops 559742976 | bytes 5513216 | tf_op jit(solution)/shard_map/transpose(jvp())/dot_general | solution.py:14
  381.7 7.5 %collective-permute-start.37 = (bf16[3,128,512]{2,1,0:T(8,128)(2,1)S(1)}, bf16[3,128,512]{2,1,0:T(8,128)(2,1)S(1)}, u32[]{:S(2)}, u32[]{:S(2)}) collective-permute-start(bf16[3,128,512]{2,1,0:T(8,128)(2,1)S(1)} %get-tuple-element.24), channel_id=1, source_target_pairs={{0,63},{1,0},{2,1},{3,2},{4,3},{5,4},{6,5},{7,6},{8,7},{9,8},{10,9... | collective-permute-start | bytes 1179656 | tf_op jit(solution)/shard_map/ppermute | solution.py:33
  390.5 7.4 %collective-permute-start.58 = (bf16[3,512,128]{2,1,0:T(8,128)(2,1)S(1)}, bf16[3,512,128]{2,1,0:T(8,128)(2,1)S(1)}, u32[]{:S(2)}, u32[]{:S(2)}) collective-permute-start(bf16[3,512,128]{2,1,0:T(8,128)(2,1)S(1)} %copy-done.174), channel_id=1, source_target_pairs={{0,63},{1,0},{2,1},{3,2},{4,3},{5,4},{6,5},{7,6},{8,7},{9,8},{10,9... | collective-permute-start | bytes 1179656 | tf_op jit(solution)/shard_map/ppermute | solution.py:33
  398.9 8.1 %collective-permute-start.55 = (bf16[3,512,128]{2,1,0:T(8,128)(2,1)S(1)}, bf16[3,512,128]{2,1,0:T(8,128)(2,1)S(1)}, u32[]{:S(2)}, u32[]{:S(2)}) collective-permute-start(bf16[3,512,128]{2,1,0:T(8,128)(2,1)S(1)} %copy-done.126), channel_id=1, source_target_pairs={{0,63},{1,0},{2,1},{3,2},{4,3},{5,4},{6,5},{7,6},{8,7},{9,8},{10,9... | collective-permute-start | bytes 1179656 | tf_op jit(solution)/shard_map/ppermute | solution.py:33
  410.9 7.4 %collective-permute-start.52 = (bf16[3,128,512]{2,1,0:T(8,128)(2,1)}, bf16[3,128,512]{2,1,0:T(8,128)(2,1)}, u32[]{:S(2)}, u32[]{:S(2)}) collective-permute-start(bf16[3,128,512]{2,1,0:T(8,128)(2,1)} %convert_element_type.1644), channel_id=1, source_target_pairs={{0,63},{1,0},{2,1},{3,2},{4,3},{5,4},{6,5},{7,6},{8,7},{9,8},{10,9... | collective-permute-start | bytes 1179656 | tf_op jit(solution)/shard_map/ppermute | solution.py:33
  443.4 7.5 %collective-permute-start.64 = (bf16[3,512,128]{2,1,0:T(8,128)(2,1)}, bf16[3,512,128]{2,1,0:T(8,128)(2,1)}, u32[]{:S(2)}, u32[]{:S(2)}) collective-permute-start(bf16[3,512,128]{2,1,0:T(8,128)(2,1)} %get-tuple-element.11), channel_id=1, source_target_pairs={{0,63},{1,0},{2,1},{3,2},{4,3},{5,4},{6,5},{7,6},{8,7},{9,8},{10,9... | collective-permute-start | bytes 1179656 | tf_op jit(solution)/shard_map/ppermute | solution.py:33
  452.9 6.3 %fusion.477 = bf16[1,128,512]{2,1,0:T(8,128)(2,1)} fusion(f32[2048,512]{1,0:T(8,128)} %get-tuple-element.112, bf16[2048,128]{0,1:T(8,128)(2,1)} %fusion.515, bf16[1,1,1,2048,128]{3,4,2,1,0:T(8,128)(2,1)S(1)} %copy-done.50, f32[2048]{0:T(1024)S(1)} %copy-done.182, bf16[3,512,128]{2,1,0:T(8,128)(2,1)} %copy-done.131), kind=kOutput, calls=%fused_computation.673 | convolution fusion | flops 559742976 | bytes 5513216 | tf_op jit(solution)/shard_map/transpose(jvp())/dot_general | solution.py:14
  464.3 7.4 %collective-permute-start.49 = (bf16[3,128,512]{2,1,0:T(8,128)(2,1)S(1)}, bf16[3,128,512]{2,1,0:T(8,128)(2,1)S(1)}, u32[]{:S(2)}, u32[]{:S(2)}) collective-permute-start(bf16[3,128,512]{2,1,0:T(8,128)(2,1)S(1)} %copy-done.72), channel_id=1, source_target_pairs={{0,63},{1,0},{2,1},{3,2},{4,3},{5,4},{6,5},{7,6},{8,7},{9,8},{10,9... | collective-permute-start | bytes 1179656 | tf_op jit(solution)/shard_map/ppermute | solution.py:33
  475.7 7.4 %collective-permute-start.61 = (bf16[3,512,128]{2,1,0:T(8,128)(2,1)S(1)}, bf16[3,512,128]{2,1,0:T(8,128)(2,1)S(1)}, u32[]{:S(2)}, u32[]{:S(2)}) collective-permute-start(bf16[3,512,128]{2,1,0:T(8,128)(2,1)S(1)} %copy-done.132), channel_id=1, source_target_pairs={{0,63},{1,0},{2,1},{3,2},{4,3},{5,4},{6,5},{7,6},{8,7},{9,8},{10,9... | collective-permute-start | bytes 1179656 | tf_op jit(solution)/shard_map/ppermute | solution.py:33
  512.3 7.4 %collective-permute-start.70 = (bf16[3,512,128]{2,1,0:T(8,128)(2,1)}, bf16[3,512,128]{2,1,0:T(8,128)(2,1)}, u32[]{:S(2)}, u32[]{:S(2)}) collective-permute-start(bf16[3,512,128]{2,1,0:T(8,128)(2,1)} %get-tuple-element.4), channel_id=1, source_target_pairs={{0,63},{1,0},{2,1},{3,2},{4,3},{5,4},{6,5},{7,6},{8,7},{9,8},{10,9... | collective-permute-start | bytes 1179656 | tf_op jit(solution)/shard_map/ppermute | solution.py:33
  520.5 7.5 %collective-permute-start.67 = (bf16[3,128,512]{2,1,0:T(8,128)(2,1)}, bf16[3,128,512]{2,1,0:T(8,128)(2,1)}, u32[]{:S(2)}, u32[]{:S(2)}) collective-permute-start(bf16[3,128,512]{2,1,0:T(8,128)(2,1)} %convert_element_type.1711), channel_id=1, source_target_pairs={{0,63},{1,0},{2,1},{3,2},{4,3},{5,4},{6,5},{7,6},{8,7},{9,8},{10,9... | collective-permute-start | bytes 1179656 | tf_op jit(solution)/shard_map/ppermute | solution.py:33
  529.9 6.3 %fusion.480 = bf16[1,128,512]{2,1,0:T(8,128)(2,1)} fusion(f32[2048,512]{1,0:T(8,128)} %get-tuple-element.122, bf16[2048,128]{0,1:T(8,128)(2,1)} %fusion.517, bf16[1,1,1,2048,128]{3,4,2,1,0:T(8,128)(2,1)S(1)} %copy-done.49, f32[2048]{0:T(1024)S(1)} %copy-done.181, bf16[3,512,128]{2,1,0:T(8,128)(2,1)} %copy-done.133), kind=kOutput, calls=%fused_computation.674 | convolution fusion | flops 559742976 | bytes 5513216 | tf_op jit(solution)/shard_map/transpose(jvp())/dot_general | solution.py:14
  (702 shorter events, 307.9 us)
Async XLA Ops:
  2.9 97.8 %collective-permute-start.10 = (bf16[3,512,128]{2,1,0:T(8,128)(2,1)}, bf16[3,512,128]{2,1,0:T(8,128)(2,1)}, u32[]{:S(2)}, u32[]{:S(2)}) collective-permute-start(bf16[3,512,128]{2,1,0:T(8,128)(2,1)} %get-tuple-element.53), channel_id=1, source_target_pairs={{0,63},{1,0},{2,1},{3,2},{4,3},{5,4},{6,5},{7,6},{8,7},{9,8},{10,9... | collective-permute-start | bytes 1179656 | tf_op jit(solution)/shard_map/ppermute | solution.py:33
  11.7 88.9 %collective-permute-start.11 = (bf16[3,512,128]{2,1,0:T(8,128)(2,1)}, bf16[3,512,128]{2,1,0:T(8,128)(2,1)}, u32[]{:S(2)}, u32[]{:S(2)}) collective-permute-start(bf16[3,512,128]{2,1,0:T(8,128)(2,1)} %get-tuple-element.53), channel_id=1, source_target_pairs={{0,64},{64,0},{1,65},{65,1},{2,66},{66,2},{3,67},{67,3},{4,68},{68... | collective-permute-start | bytes 1179656 | tf_op jit(solution)/shard_map/ppermute | solution.py:33
  14.0 78.7 %collective-permute-start = (bf16[3,128,512]{2,1,0:T(8,128)(2,1)}, bf16[3,128,512]{2,1,0:T(8,128)(2,1)}, u32[]{:S(2)}, u32[]{:S(2)}) collective-permute-start(bf16[3,128,512]{2,1,0:T(8,128)(2,1)} %get-tuple-element.55), channel_id=1, source_target_pairs={{0,1},{1,2},{2,3},{3,4},{4,5},{5,6},{6,7},{7,8},{8,9},{9,10},{10,1... | collective-permute-start | bytes 1179656 | tf_op jit(solution)/shard_map/ppermute | solution.py:33
  14.0 79.3 %collective-permute-start.1 = (bf16[3,128,512]{2,1,0:T(8,128)(2,1)}, bf16[3,128,512]{2,1,0:T(8,128)(2,1)}, u32[]{:S(2)}, u32[]{:S(2)}) collective-permute-start(bf16[3,128,512]{2,1,0:T(8,128)(2,1)} %get-tuple-element.55), channel_id=1, source_target_pairs={{0,63},{1,0},{2,1},{3,2},{4,3},{5,4},{6,5},{7,6},{8,7},{9,8},{10,9... | collective-permute-start | bytes 1179656 | tf_op jit(solution)/shard_map/ppermute | solution.py:33
  21.4 71.9 %collective-permute-start.2 = (bf16[3,128,512]{2,1,0:T(8,128)(2,1)}, bf16[3,128,512]{2,1,0:T(8,128)(2,1)}, u32[]{:S(2)}, u32[]{:S(2)}) collective-permute-start(bf16[3,128,512]{2,1,0:T(8,128)(2,1)} %get-tuple-element.55), channel_id=1, source_target_pairs={{0,64},{64,0},{1,65},{65,1},{2,66},{66,2},{3,67},{67,3},{4,68},{68... | collective-permute-start | bytes 1179656 | tf_op jit(solution)/shard_map/ppermute | solution.py:33
  134.1 27.6 %collective-permute-start.21 = (bf16[3,512,128]{2,1,0:T(8,128)(2,1)}, bf16[3,512,128]{2,1,0:T(8,128)(2,1)}, u32[]{:S(2)}, u32[]{:S(2)}) collective-permute-start(bf16[3,512,128]{2,1,0:T(8,128)(2,1)} %get-tuple-element.57), channel_id=1, source_target_pairs={{0,1},{1,2},{2,3},{3,4},{4,5},{5,6},{6,7},{7,8},{8,9},{9,10},{10,1... | collective-permute-start | bytes 1179656 | tf_op jit(solution)/shard_map/ppermute | solution.py:33
  134.2 27.6 %collective-permute-start.22 = (bf16[3,512,128]{2,1,0:T(8,128)(2,1)}, bf16[3,512,128]{2,1,0:T(8,128)(2,1)}, u32[]{:S(2)}, u32[]{:S(2)}) collective-permute-start(bf16[3,512,128]{2,1,0:T(8,128)(2,1)} %get-tuple-element.57), channel_id=1, source_target_pairs={{0,63},{1,0},{2,1},{3,2},{4,3},{5,4},{6,5},{7,6},{8,7},{9,8},{10,9... | collective-permute-start | bytes 1179656 | tf_op jit(solution)/shard_map/ppermute | solution.py:33
  141.7 27.8 %collective-permute-start.3 = (bf16[3,128,512]{2,1,0:T(8,128)(2,1)}, bf16[3,128,512]{2,1,0:T(8,128)(2,1)}, u32[]{:S(2)}, u32[]{:S(2)}) collective-permute-start(bf16[3,128,512]{2,1,0:T(8,128)(2,1)} %get-tuple-element.60), channel_id=1, source_target_pairs={{0,1},{1,2},{2,3},{3,4},{4,5},{5,6},{6,7},{7,8},{8,9},{9,10},{10,1... | collective-permute-start | bytes 1179656 | tf_op jit(solution)/shard_map/ppermute | solution.py:33
  141.7 30.9 %collective-permute-start.4 = (bf16[3,128,512]{2,1,0:T(8,128)(2,1)}, bf16[3,128,512]{2,1,0:T(8,128)(2,1)}, u32[]{:S(2)}, u32[]{:S(2)}) collective-permute-start(bf16[3,128,512]{2,1,0:T(8,128)(2,1)} %get-tuple-element.60), channel_id=1, source_target_pairs={{0,63},{1,0},{2,1},{3,2},{4,3},{5,4},{6,5},{7,6},{8,7},{9,8},{10,9... | collective-permute-start | bytes 1179656 | tf_op jit(solution)/shard_map/ppermute | solution.py:33
  211.2 28.5 %collective-permute-start.33 = (bf16[3,512,128]{2,1,0:T(8,128)(2,1)}, bf16[3,512,128]{2,1,0:T(8,128)(2,1)}, u32[]{:S(2)}, u32[]{:S(2)}) collective-permute-start(bf16[3,512,128]{2,1,0:T(8,128)(2,1)} %get-tuple-element.29), channel_id=1, source_target_pairs={{0,1},{1,2},{2,3},{3,4},{4,5},{5,6},{6,7},{7,8},{8,9},{9,10},{10,1... | collective-permute-start | bytes 1179656 | tf_op jit(solution)/shard_map/ppermute | solution.py:33
  211.3 28.5 %collective-permute-start.34 = (bf16[3,512,128]{2,1,0:T(8,128)(2,1)}, bf16[3,512,128]{2,1,0:T(8,128)(2,1)}, u32[]{:S(2)}, u32[]{:S(2)}) collective-permute-start(bf16[3,512,128]{2,1,0:T(8,128)(2,1)} %get-tuple-element.29), channel_id=1, source_target_pairs={{0,63},{1,0},{2,1},{3,2},{4,3},{5,4},{6,5},{7,6},{8,7},{9,8},{10,9... | collective-permute-start | bytes 1179656 | tf_op jit(solution)/shard_map/ppermute | solution.py:33
  218.7 21.2 %collective-permute-start.35 = (bf16[3,512,128]{2,1,0:T(8,128)(2,1)}, bf16[3,512,128]{2,1,0:T(8,128)(2,1)}, u32[]{:S(2)}, u32[]{:S(2)}) collective-permute-start(bf16[3,512,128]{2,1,0:T(8,128)(2,1)} %get-tuple-element.29), channel_id=1, source_target_pairs={{0,64},{64,0},{1,65},{65,1},{2,66},{66,2},{3,67},{67,3},{4,68},{68... | collective-permute-start | bytes 1179656 | tf_op jit(solution)/shard_map/ppermute | solution.py:33
  219.5 27.8 %collective-permute-start.15 = (bf16[3,128,512]{2,1,0:T(8,128)(2,1)}, bf16[3,128,512]{2,1,0:T(8,128)(2,1)}, u32[]{:S(2)}, u32[]{:S(2)}) collective-permute-start(bf16[3,128,512]{2,1,0:T(8,128)(2,1)} %convert_element_type.1461), channel_id=1, source_target_pairs={{0,1},{1,2},{2,3},{3,4},{4,5},{5,6},{6,7},{7,8},{8,9},{9,10},{10,1... | collective-permute-start | bytes 1179656 | tf_op jit(solution)/shard_map/ppermute | solution.py:33
  219.5 31.6 %collective-permute-start.16 = (bf16[3,128,512]{2,1,0:T(8,128)(2,1)}, bf16[3,128,512]{2,1,0:T(8,128)(2,1)}, u32[]{:S(2)}, u32[]{:S(2)}) collective-permute-start(bf16[3,128,512]{2,1,0:T(8,128)(2,1)} %convert_element_type.1461), channel_id=1, source_target_pairs={{0,63},{1,0},{2,1},{3,2},{4,3},{5,4},{6,5},{7,6},{8,7},{9,8},{10,9... | collective-permute-start | bytes 1179656 | tf_op jit(solution)/shard_map/ppermute | solution.py:33
  287.2 27.6 %collective-permute-start.45 = (bf16[3,512,128]{2,1,0:T(8,128)(2,1)}, bf16[3,512,128]{2,1,0:T(8,128)(2,1)}, u32[]{:S(2)}, u32[]{:S(2)}) collective-permute-start(bf16[3,512,128]{2,1,0:T(8,128)(2,1)} %get-tuple-element.22), channel_id=1, source_target_pairs={{0,1},{1,2},{2,3},{3,4},{4,5},{5,6},{6,7},{7,8},{8,9},{9,10},{10,1... | collective-permute-start | bytes 1179656 | tf_op jit(solution)/shard_map/ppermute | solution.py:33
  287.3 27.6 %collective-permute-start.46 = (bf16[3,512,128]{2,1,0:T(8,128)(2,1)}, bf16[3,512,128]{2,1,0:T(8,128)(2,1)}, u32[]{:S(2)}, u32[]{:S(2)}) collective-permute-start(bf16[3,512,128]{2,1,0:T(8,128)(2,1)} %get-tuple-element.22), channel_id=1, source_target_pairs={{0,63},{1,0},{2,1},{3,2},{4,3},{5,4},{6,5},{7,6},{8,7},{9,8},{10,9... | collective-permute-start | bytes 1179656 | tf_op jit(solution)/shard_map/ppermute | solution.py:33
  295.5 26.9 %collective-permute-start.27 = (bf16[3,128,512]{2,1,0:T(8,128)(2,1)}, bf16[3,128,512]{2,1,0:T(8,128)(2,1)}, u32[]{:S(2)}, u32[]{:S(2)}) collective-permute-start(bf16[3,128,512]{2,1,0:T(8,128)(2,1)} %convert_element_type.1522), channel_id=1, source_target_pairs={{0,1},{1,2},{2,3},{3,4},{4,5},{5,6},{6,7},{7,8},{8,9},{9,10},{10,1... | collective-permute-start | bytes 1179656 | tf_op jit(solution)/shard_map/ppermute | solution.py:33
  295.5 30.1 %collective-permute-start.28 = (bf16[3,128,512]{2,1,0:T(8,128)(2,1)}, bf16[3,128,512]{2,1,0:T(8,128)(2,1)}, u32[]{:S(2)}, u32[]{:S(2)}) collective-permute-start(bf16[3,128,512]{2,1,0:T(8,128)(2,1)} %convert_element_type.1522), channel_id=1, source_target_pairs={{0,63},{1,0},{2,1},{3,2},{4,3},{5,4},{6,5},{7,6},{8,7},{9,8},{10,9... | collective-permute-start | bytes 1179656 | tf_op jit(solution)/shard_map/ppermute | solution.py:33
  356.9 32.9 %collective-permute-start.39 = (bf16[3,128,512]{2,1,0:T(8,128)(2,1)}, bf16[3,128,512]{2,1,0:T(8,128)(2,1)}, u32[]{:S(2)}, u32[]{:S(2)}) collective-permute-start(bf16[3,128,512]{2,1,0:T(8,128)(2,1)} %convert_element_type.1583), channel_id=1, source_target_pairs={{0,1},{1,2},{2,3},{3,4},{4,5},{5,6},{6,7},{7,8},{8,9},{9,10},{10,1... | collective-permute-start | bytes 1179656 | tf_op jit(solution)/shard_map/ppermute | solution.py:33
  356.9 33.5 %collective-permute-start.40 = (bf16[3,128,512]{2,1,0:T(8,128)(2,1)}, bf16[3,128,512]{2,1,0:T(8,128)(2,1)}, u32[]{:S(2)}, u32[]{:S(2)}) collective-permute-start(bf16[3,128,512]{2,1,0:T(8,128)(2,1)} %convert_element_type.1583), channel_id=1, source_target_pairs={{0,63},{1,0},{2,1},{3,2},{4,3},{5,4},{6,5},{7,6},{8,7},{9,8},{10,9... | collective-permute-start | bytes 1179656 | tf_op jit(solution)/shard_map/ppermute | solution.py:33
  364.3 26.1 %collective-permute-start.41 = (bf16[3,128,512]{2,1,0:T(8,128)(2,1)}, bf16[3,128,512]{2,1,0:T(8,128)(2,1)}, u32[]{:S(2)}, u32[]{:S(2)}) collective-permute-start(bf16[3,128,512]{2,1,0:T(8,128)(2,1)} %convert_element_type.1583), channel_id=1, source_target_pairs={{0,64},{64,0},{1,65},{65,1},{2,66},{66,2},{3,67},{67,3},{4,68},{68... | collective-permute-start | bytes 1179656 | tf_op jit(solution)/shard_map/ppermute | solution.py:33
  364.3 33.6 %collective-permute-start.36 = (bf16[3,128,512]{2,1,0:T(8,128)(2,1)S(1)}, bf16[3,128,512]{2,1,0:T(8,128)(2,1)}, u32[]{:S(2)}, u32[]{:S(2)}) collective-permute-start(bf16[3,128,512]{2,1,0:T(8,128)(2,1)S(1)} %get-tuple-element.24), channel_id=1, source_target_pairs={{0,1},{1,2},{2,3},{3,4},{4,5},{5,6},{6,7},{7,8},{8,9},{9,10},{10,1... | collective-permute-start | bytes 1179656 | tf_op jit(solution)/shard_map/ppermute | solution.py:33
  398.8 24.3 %collective-permute-start.54 = (bf16[3,512,128]{2,1,0:T(8,128)(2,1)S(1)}, bf16[3,512,128]{2,1,0:T(8,128)(2,1)S(1)}, u32[]{:S(2)}, u32[]{:S(2)}) collective-permute-start(bf16[3,512,128]{2,1,0:T(8,128)(2,1)S(1)} %copy-done.126), channel_id=1, source_target_pairs={{0,1},{1,2},{2,3},{3,4},{4,5},{5,6},{6,7},{7,8},{8,9},{9,10},{10,1... | collective-permute-start | bytes 1179656 | tf_op jit(solution)/shard_map/ppermute | solution.py:33
  398.9 24.2 %collective-permute-start.55 = (bf16[3,512,128]{2,1,0:T(8,128)(2,1)S(1)}, bf16[3,512,128]{2,1,0:T(8,128)(2,1)S(1)}, u32[]{:S(2)}, u32[]{:S(2)}) collective-permute-start(bf16[3,512,128]{2,1,0:T(8,128)(2,1)S(1)} %copy-done.126), channel_id=1, source_target_pairs={{0,63},{1,0},{2,1},{3,2},{4,3},{5,4},{6,5},{7,6},{8,7},{9,8},{10,9... | collective-permute-start | bytes 1179656 | tf_op jit(solution)/shard_map/ppermute | solution.py:33
  410.8 52.9 %collective-permute-start.51 = (bf16[3,128,512]{2,1,0:T(8,128)(2,1)}, bf16[3,128,512]{2,1,0:T(8,128)(2,1)}, u32[]{:S(2)}, u32[]{:S(2)}) collective-permute-start(bf16[3,128,512]{2,1,0:T(8,128)(2,1)} %convert_element_type.1644), channel_id=1, source_target_pairs={{0,1},{1,2},{2,3},{3,4},{4,5},{5,6},{6,7},{7,8},{8,9},{9,10},{10,1... | collective-permute-start | bytes 1179656 | tf_op jit(solution)/shard_map/ppermute | solution.py:33
  410.9 64.7 %collective-permute-start.52 = (bf16[3,128,512]{2,1,0:T(8,128)(2,1)}, bf16[3,128,512]{2,1,0:T(8,128)(2,1)}, u32[]{:S(2)}, u32[]{:S(2)}) collective-permute-start(bf16[3,128,512]{2,1,0:T(8,128)(2,1)} %convert_element_type.1644), channel_id=1, source_target_pairs={{0,63},{1,0},{2,1},{3,2},{4,3},{5,4},{6,5},{7,6},{8,7},{9,8},{10,9... | collective-permute-start | bytes 1179656 | tf_op jit(solution)/shard_map/ppermute | solution.py:33
  450.8 20.9 %collective-permute-start.65 = (bf16[3,512,128]{2,1,0:T(8,128)(2,1)}, bf16[3,512,128]{2,1,0:T(8,128)(2,1)}, u32[]{:S(2)}, u32[]{:S(2)}) collective-permute-start(bf16[3,512,128]{2,1,0:T(8,128)(2,1)} %get-tuple-element.11), channel_id=1, source_target_pairs={{0,64},{64,0},{1,65},{65,1},{2,66},{66,2},{3,67},{67,3},{4,68},{68... | collective-permute-start | bytes 1179656 | tf_op jit(solution)/shard_map/ppermute | solution.py:33
  512.2 28.4 %collective-permute-start.69 = (bf16[3,512,128]{2,1,0:T(8,128)(2,1)}, bf16[3,512,128]{2,1,0:T(8,128)(2,1)}, u32[]{:S(2)}, u32[]{:S(2)}) collective-permute-start(bf16[3,512,128]{2,1,0:T(8,128)(2,1)} %get-tuple-element.4), channel_id=1, source_target_pairs={{0,1},{1,2},{2,3},{3,4},{4,5},{5,6},{6,7},{7,8},{8,9},{9,10},{10,1... | collective-permute-start | bytes 1179656 | tf_op jit(solution)/shard_map/ppermute | solution.py:33
  512.3 29.2 %collective-permute-start.70 = (bf16[3,512,128]{2,1,0:T(8,128)(2,1)}, bf16[3,512,128]{2,1,0:T(8,128)(2,1)}, u32[]{:S(2)}, u32[]{:S(2)}) collective-permute-start(bf16[3,512,128]{2,1,0:T(8,128)(2,1)} %get-tuple-element.4), channel_id=1, source_target_pairs={{0,63},{1,0},{2,1},{3,2},{4,3},{5,4},{6,5},{7,6},{8,7},{9,8},{10,9... | collective-permute-start | bytes 1179656 | tf_op jit(solution)/shard_map/ppermute | solution.py:33
  519.7 21.7 %collective-permute-start.71 = (bf16[3,512,128]{2,1,0:T(8,128)(2,1)}, bf16[3,512,128]{2,1,0:T(8,128)(2,1)}, u32[]{:S(2)}, u32[]{:S(2)}) collective-permute-start(bf16[3,512,128]{2,1,0:T(8,128)(2,1)} %get-tuple-element.4), channel_id=1, source_target_pairs={{0,64},{64,0},{1,65},{65,1},{2,66},{66,2},{3,67},{67,3},{4,68},{68... | collective-permute-start | bytes 1179656 | tf_op jit(solution)/shard_map/ppermute | solution.py:33
  520.5 23.5 %collective-permute-start.66 = (bf16[3,128,512]{2,1,0:T(8,128)(2,1)}, bf16[3,128,512]{2,1,0:T(8,128)(2,1)}, u32[]{:S(2)}, u32[]{:S(2)}) collective-permute-start(bf16[3,128,512]{2,1,0:T(8,128)(2,1)} %convert_element_type.1711), channel_id=1, source_target_pairs={{0,1},{1,2},{2,3},{3,4},{4,5},{5,6},{6,7},{7,8},{8,9},{9,10},{10,1... | collective-permute-start | bytes 1179656 | tf_op jit(solution)/shard_map/ppermute | solution.py:33
  520.5 23.5 %collective-permute-start.67 = (bf16[3,128,512]{2,1,0:T(8,128)(2,1)}, bf16[3,128,512]{2,1,0:T(8,128)(2,1)}, u32[]{:S(2)}, u32[]{:S(2)}) collective-permute-start(bf16[3,128,512]{2,1,0:T(8,128)(2,1)} %convert_element_type.1711), channel_id=1, source_target_pairs={{0,63},{1,0},{2,1},{3,2},{4,3},{5,4},{6,5},{7,6},{8,7},{9,8},{10,9... | collective-permute-start | bytes 1179656 | tf_op jit(solution)/shard_map/ppermute | solution.py:33
  (230 other events, 3102.3 us)
where the time goes:
time: 558 us; the launch traced here: 547 us
  matrix products  236 us (42%)
  starting transfers between devices  185 us (33%)
  other arithmetic  64.1 us (11%)
  local copies, waits for them, and re-layouts  35 us (6%)
  waiting for transfers between devices  22.8 us (4%)
    ppermute x72, starting transfers between devices, neighbour_shift(): return lax.ppermute(values, axis_name, perm_pairs)  185 us
    dot_general x56, matrix products, layer_step(): jnp.dot(normed, mat_in.astype(jnp.bfloat16), preferred_element_type=jnp.f...  120 us
    dot_general x56, matrix products, layer_step(): jnp.dot(gelu_out, mat_out.astype(jnp.bfloat16), preferred_element_type=jn...  116 us
    convert_element_type x18, other arithmetic, gossip_mix(): sent_copy = values.astype(jnp.bfloat16)  35.4 us
    unnamed x394, local copies, waits for them, and re-layouts  29.6 us
    ppermute x72, waiting for transfers between devices, neighbour_shift(): return lax.ppermute(values, axis_name, perm_pairs)  22.8 us
  transfers between devices with their start and end apart: 72, of which 5 were waited for; matrix products, arithmetic and copies ran while one was open for 42% of the time, Pallas kernels for 0%

commit v1 on v0

v1 whole, which is shorter than its diff:
```python
import functools

import jax
import jax.numpy as jnp
from jax import lax
from jax.experimental import pallas as pl
from jax.experimental.pallas import tpu as pltpu
from jax.sharding import PartitionSpec as P

EPS = 1e-6
LEARN_RATE = 0.125
F32 = jnp.float32
BF16 = jnp.bfloat16
C0 = 0.7978845608028654
C1 = 0.7978845608028654 * 0.044715
TILE = 256


def dot(a, b, dims):
    return lax.dot_general(a, b, (dims, ((), ())), preferred_element_type=F32)


def forward_tile(rows, h_in, win, wout, u_ref, inv_ref, gp_ref, a_ref):
    d = h_in.shape[-1]
    hf = h_in[rows, :].astype(F32)
    ms = jnp.sum(hf * hf, axis=-1, keepdims=True) * (1.0 / d)
    inv = jnp.broadcast_to(lax.rsqrt(ms + EPS), hf.shape)
    inv_ref[rows, :] = inv
    u = (hf * inv).astype(BF16)
    u_ref[rows, :] = u
    z = dot(u, win[...], ((1,), (0,)))
    z2 = z * z
    t = jnp.tanh(z * (C0 + C1 * z2))
    w = 0.5 + 0.5 * t
    a = (z * w).astype(BF16)
    a_ref[rows, :] = a
    gp_ref[rows, :] = w + (w - w * w) * (z * (2.0 * C0 + (6.0 * C1) * z2))
    mlp = dot(a, wout[...], ((1,), (0,)))
    return (hf + mlp).astype(BF16)


def backward_tile(rows, first, h_in, win, wout, u_ref, inv_ref, gp_ref, a_ref, dh_ref, dwin, dwoutt):
    d = dh_ref[rows, :]
    da = dot(d, wout[...], ((1,), (1,))).astype(BF16).astype(F32)
    dz = (da * gp_ref[rows, :]).astype(BF16)
    dwoutt[...] += dot(d, a_ref[rows, :], ((0,), (0,)))
    dwin[...] += dot(u_ref[rows, :], dz, ((0,), (0,)))
    if not first:
        du = dot(dz, win[...], ((1,), (1,))).astype(BF16).astype(F32)
        hf = h_in[rows, :].astype(F32)
        inv = inv_ref[rows, :]
        s = jnp.sum(du * hf, axis=-1, keepdims=True) * (-1.0 / hf.shape[-1])
        dhf = d.astype(F32) + du * inv + hf * (inv * inv * inv * s)
        dh_ref[rows, :] = dhf.astype(BF16)


def kernel(dims, w_in, w_out, x_hbm, t_hbm, o_pin, o_pout, o_yin, o_yout,
           p_in, p_out, y_in, y_out, pb_in, pb_out, yb_in, yb_out, r_in, r_out, g_in, g_out,
           dw_in, dw_outt, xb, tb, hid, u_all, inv_all, gp_all, a_all, dh,
           lsem, xsem, ssem, rsem):
    size_x, size_y, layers, steps = dims
    rows_n = xb.shape[1]
    me_x = lax.axis_index('tx')
    me_y = lax.axis_index('ty')
    right = lax.rem(me_x + 1, size_x)
    left = lax.rem(me_x + size_x - 1, size_x)
    other = lax.rem(me_y + 1, size_y)
    peers = ({'tx': right, 'ty': me_y}, {'tx': left, 'ty': me_y}, {'tx': me_x, 'ty': other})
    chunks = [(l, k) for l in range(layers) for k in range(2)]
    pst, yst, pbs, ybs, rcv, gold = (p_in, p_out), (y_in, y_out), (pb_in, pb_out), (yb_in, yb_out), (r_in, r_out), (g_in, g_out)

    def loads():
        return [pltpu.make_async_copy(w_in, p_in, lsem.at[0]), pltpu.make_async_copy(w_out, p_out, lsem.at[1])]

    def batch(t, slot):
        return [pltpu.make_async_copy(x_hbm.at[t], xb.at[slot], xsem.at[slot, 0]),
                pltpu.make_async_copy(t_hbm.at[t], tb.at[slot], xsem.at[slot, 1])]

    def send(kind, par, c, d):
        l, k = chunks[c]
        src = (pbs, ybs)[kind][k].at[l]
        return pltpu.make_async_remote_copy(
            src_ref=src, dst_ref=rcv[k].at[kind, par, d, l], send_sem=ssem.at[kind, d, c],
            recv_sem=rsem.at[kind, par, d, c], device_id=peers[d], device_id_type=pl.DeviceIdType.MESH)

    def start_sends(kind, par, c):
        for d in range(3):
            send(kind, par, c, d).start()

    def wait_chunk(kind, par, c):
        for d in range(3):
            send(kind, par, c, d).wait()

    def mix(v, kind, par, l, k, sl):
        s = v + rcv[k][kind, par, 0, l, sl, :].astype(F32)
        s = s + rcv[k][kind, par, 1, l, sl, :].astype(F32)
        n = rcv[k][kind, par, 2, l, sl, :].astype(F32)
        return (s + n + n) * 0.2

    for cp in loads() + batch(0, 0):
        cp.start()
    barrier = pltpu.get_barrier_semaphore()
    for peer in peers:
        pl.semaphore_signal(barrier, inc=1, device_id=peer, device_id_type=pl.DeviceIdType.MESH)
    for cp in loads():
        cp.wait()
    for l, k in chunks:
        pbs[k][l] = pst[k][l].astype(BF16)
    pl.semaphore_wait(barrier, 3)
    for c in range(len(chunks)):
        start_sends(0, 0, c)

    def step(t, carry):
        slot = lax.rem(t, 2)
        nxt = 1 - slot
        for cp in batch(t, slot):
            cp.wait()

        @pl.when(t < steps)
        def _():
            for cp in batch(t + 1, nxt):
                cp.start()

        tiles = rows_n // TILE
        for l in range(layers):
            h_in = xb.at[slot] if l == 0 else hid.at[l - 1]

            def fwd(i, c, l=l, h_in=h_in):
                rows = pl.ds(pl.multiple_of(i * TILE, TILE), TILE)
                h = forward_tile(rows, h_in, pb_in.at[l], pb_out.at[l], u_all.at[l], inv_all.at[l], gp_all.at[l], a_all.at[l])
                if l + 1 < layers:
                    hid[l, rows, :] = h
                else:
                    err = h.astype(F32) - tb[slot, rows, :].astype(F32)
                    dh[rows, :] = (err * (2.0 / (rows_n * h.shape[-1]))).astype(BF16)
                return c

            lax.fori_loop(0, tiles, fwd, 0)
        for l in reversed(range(layers)):
            h_in = xb.at[slot] if l == 0 else hid.at[l - 1]
            dw_in[l] = jnp.zeros_like(dw_in[l])
            dw_outt[l] = jnp.zeros_like(dw_outt[l])

            def bwd(i, c, l=l, h_in=h_in):
                rows = pl.ds(pl.multiple_of(i * TILE, TILE), TILE)
                backward_tile(rows, l == 0, h_in, pb_in.at[l], pb_out.at[l], u_all.at[l], inv_all.at[l], gp_all.at[l],
                              a_all.at[l], dh, dw_in.at[l], dw_outt.at[l])
                return c

            lax.fori_loop(0, tiles, bwd, 0)

        def new_grad(l, k):
            g = dw_in[l] if k == 0 else dw_outt[l].T
            return g.astype(BF16).astype(F32)

        for c, (l, k) in enumerate(chunks):
            g = new_grad(l, k)

            @pl.when(t == 0)
            def _():
                yst[k][l] = g

            @pl.when(t > 0)
            def _():
                wait_chunk(1, nxt, c)
                yst[k][l] = (mix(yst[k][l], 1, nxt, l, k, slice(None)) + g) - gold[k][l].astype(F32)

            gold[k][l] = g.astype(BF16)

            @pl.when(t < steps)
            def _():
                ybs[k][l] = yst[k][l].astype(BF16)
                if c > 0:
                    start_sends(1, slot, c - 1)

        @pl.when(t < steps)
        def _():
            for c, (l, k) in enumerate(chunks):
                wait_chunk(0, slot, c)
                pn = mix(pst[k][l], 0, slot, l, k, slice(None)) - LEARN_RATE * yst[k][l]
                pst[k][l] = pn
                pbs[k][l] = pn.astype(BF16)
                if c == 0:
                    start_sends(1, slot, len(chunks) - 1)
                else:
                    @pl.when(t < steps - 1)
                    def _():
                        start_sends(0, nxt, c - 1)

            @pl.when(t < steps - 1)
            def _():
                start_sends(0, nxt, len(chunks) - 1)

            @pl.when(t == steps - 1)
            def _():
                for cp in outs_p():
                    cp.start()
        return carry

    def outs_p():
        return [pltpu.make_async_copy(p_in, o_pin, lsem.at[0]), pltpu.make_async_copy(p_out, o_pout, lsem.at[1])]

    lax.fori_loop(0, steps + 1, step, 0)
    outs_y = [pltpu.make_async_copy(y_in, o_yin, lsem.at[2]), pltpu.make_async_copy(y_out, o_yout, lsem.at[3])]
    for cp in outs_y:
        cp.start()
    for cp in outs_p() + outs_y:
        cp.wait()


def solution(mesh):
    size_x = mesh.shape['tx']
    size_y = mesh.shape['ty']

    def device_fn(w_in, w_out, inputs, targets):
        _, _, layers, d, ff = w_in.shape
        steps = inputs.shape[2] - 1
        rows = inputs.shape[3]
        si, so = (layers, d, ff), (layers, ff, d)
        vm = pltpu.VMEM
        sem = pltpu.SemaphoreType.DMA
        any_spec = pl.BlockSpec(memory_space=pl.ANY)
        outs = pl.pallas_call(
            functools.partial(kernel, (size_x, size_y, layers, steps)),
            out_shape=[jax.ShapeDtypeStruct(si, F32), jax.ShapeDtypeStruct(so, F32)] * 2,
            in_specs=[any_spec] * 4,
            out_specs=[any_spec] * 4,
            scratch_shapes=[
                vm(si, F32), vm(so, F32), vm(si, F32), vm(so, F32),
                vm(si, BF16), vm(so, BF16), vm(si, BF16), vm(so, BF16),
                vm((2, 2, 3) + si, BF16), vm((2, 2, 3) + so, BF16), vm(si, BF16), vm(so, BF16),
                vm(si, F32), vm(si, F32),
                vm((2, rows, d), BF16), vm((2, rows, d), BF16), vm((layers - 1, rows, d), BF16),
                vm((layers, rows, d), BF16), vm((layers, rows, d), F32), vm((layers, rows, ff), F32),
                vm((layers, rows, ff), BF16), vm((rows, d), BF16),
                sem((4,)), sem((2, 2)), sem((2, 3, 2 * layers)), sem((2, 2, 3, 2 * layers)),
            ],
            compiler_params=pltpu.CompilerParams(collective_id=0, has_side_effects=True, vmem_limit_bytes=64000000),
        )(w_in[0, 0], w_out[0, 0], inputs[0, 0], targets[0, 0])
        return tuple(o[None, None] for o in outs)

    block_spec = P('tx', 'ty')
    return jax.shard_map(device_fn, mesh=mesh, in_specs=(block_spec,) * 4, out_specs=(block_spec,) * 4, check_vma=False)
```

time: 558 us -> 248 us (0.44); the launches traced: 547 us -> 248 us
  Pallas kernels: 0 us -> 242 us
  matrix products: 236 us -> 0 us
  starting transfers between devices: 185 us -> 0 us
  other arithmetic: 64.1 us -> 0 us
  local copies, waits for them, and re-layouts: 35 us -> 6.01 us
  waiting for transfers between devices: 22.8 us -> 0 us
    pallas_call x0 -> x1, Pallas kernels: none -> 242 us  [device_fn(): pl.pallas_call(functools.partial(kernel, (size_x, size_y, layers, steps))...]
    dot_general x112 -> x0, matrix products: 236 us -> none  [the longest x56 120 us: layer_step(): jnp.dot(normed, mat_in.astype(jnp.bfloat16), preferred_element_type=jnp.f...]
    ppermute x72 -> x0, starting transfers between devices: 185 us -> none  [neighbour_shift(): return lax.ppermute(values, axis_name, perm_pairs)]
    convert_element_type x32 -> x0, other arithmetic: 41.6 us -> none  [the longest x18 35.4 us: gossip_mix(): sent_copy = values.astype(jnp.bfloat16)]
    unnamed x394 -> x8, local copies, waits for them, and re-layouts: 29.6 us -> 6.01 us
    ppermute x72 -> x0, waiting for transfers between devices: 22.8 us -> none  [neighbour_shift(): return lax.ppermute(values, axis_name, perm_pairs)]
    another operation x6 -> x0, other arithmetic: 10.3 us -> none
  transfers between devices with their start and end apart: 72 -> 0, of which waited for: 5 -> 0; matrix products, arithmetic and copies ran while one was open for 42% -> 0% of each run, Pallas kernels for 0% -> 0%
where the time goes in v1:
time: 248 us
  Pallas kernels  242 us (98%)
  local copies, waits for them, and re-layouts  6.01 us (2%)
    pallas_call x1, Pallas kernels, device_fn(): pl.pallas_call(functools.partial(kernel, (size_x, size_y, layers, steps))...  242 us
    unnamed x8, local copies, waits for them, and re-layouts  6.01 us

profile of v1, /device:TPU:0, one launch (start us, length us, event | category | flops | bytes accessed | tf_op | source)
XLA Modules:
  0.0 248.3 jit_solution(2797259389375478151)
XLA Ops:
  0.6 241.6 %shard_map.75 = (f32[3,128,512]{2,1,0:T(8,128)}, f32[3,512,128]{2,1,0:T(8,128)}, f32[3,128,512]{2,1,0:T(8,128)}, f32[3,512,128]{2,1,0:T(8,128)}) custom-call(f32[3,128,512]{2,1,0:T(8,128)} %bitcast.10, f32[3,512,128]{2,1,0:T(8,128)} %bitcast.11, bf16[7,2048,128]{2,1,0:T(8,128)(2,1)} %bitcast.8, bf16[7,2048,128]{2,1,0:T(8,128)(2,1)} %bitcast.9), custom_call_target="tpu_custom_call" | custom-call | tf_op jit(solution)/shard_map/pallas_call | solution.py:223
  242.3 0.0 copy-start.1
  242.3 0.0 copy-start
  242.3 2.2 copy.12
  244.5 2.1 copy.13
  246.5 0.0 copy-done.1
  246.5 0.9 copy.14
  247.4 0.0 copy-done
  247.4 0.9 copy.15
Async XLA Ops:
  242.3 4.3 %copy-start.1 = (f32[3,128,512]{2,1,0:T(8,128)S(1)}, f32[3,128,512]{2,1,0:T(8,128)}, u32[]{:S(2)}) copy-start(f32[3,128,512]{2,1,0:T(8,128)} %get-tuple-element.10) | copy-start | bytes 2359300
  242.3 5.1 %copy-start = (f32[3,512,128]{2,1,0:T(8,128)S(1)}, f32[3,512,128]{2,1,0:T(8,128)}, u32[]{:S(2)}) copy-start(f32[3,512,128]{2,1,0:T(8,128)} %get-tuple-element.11) | copy-start | bytes 2359300

commit v2 on v1

--- a/solution.py
+++ b/solution.py
@@ -13,7 +13,7 @@
 BF16 = jnp.bfloat16
 C0 = 0.7978845608028654
 C1 = 0.7978845608028654 * 0.044715
-TILE = 256
+TILE = 1024
 
 
 def dot(a, b, dims):
@@ -54,8 +54,7 @@
         dh_ref[rows, :] = dhf.astype(BF16)
 
 
-def kernel(dims, w_in, w_out, x_hbm, t_hbm, o_pin, o_pout, o_yin, o_yout,
-           p_in, p_out, y_in, y_out, pb_in, pb_out, yb_in, yb_out, r_in, r_out, g_in, g_out,
+def kernel(dims, w_in, w_out, x_hbm, t_hbm, p_in, p_out, y_in, y_out, pb_in, pb_out, yb_in, yb_out, r_in, r_out, g_in, g_out,
            dw_in, dw_outt, xb, tb, hid, u_all, inv_all, gp_all, a_all, dh,
            lsem, xsem, ssem, rsem):
     size_x, size_y, layers, steps = dims
@@ -190,21 +189,16 @@
             @pl.when(t < steps - 1)
             def _():
                 start_sends(0, nxt, len(chunks) - 1)
-
-            @pl.when(t == steps - 1)
-            def _():
-                for cp in outs_p():
-                    cp.start()
         return carry
 
-    def outs_p():
-        return [pltpu.make_async_copy(p_in, o_pin, lsem.at[0]), pltpu.make_async_copy(p_out, o_pout, lsem.at[1])]
-
     lax.fori_loop(0, steps + 1, step, 0)
-    outs_y = [pltpu.make_async_copy(y_in, o_yin, lsem.at[2]), pltpu.make_async_copy(y_out, o_yout, lsem.at[3])]
-    for cp in outs_y:
+
+
+def flush(*refs):
+    copies = [pltpu.make_async_copy(refs[n], refs[4 + n], refs[8].at[n]) for n in range(4)]
+    for cp in copies:
         cp.start()
-    for cp in outs_p() + outs_y:
+    for cp in copies:
         cp.wait()
 
 
@@ -222,21 +216,27 @@
         any_spec = pl.BlockSpec(memory_space=pl.ANY)
         outs = pl.pallas_call(
             functools.partial(kernel, (size_x, size_y, layers, steps)),
-            out_shape=[jax.ShapeDtypeStruct(si, F32), jax.ShapeDtypeStruct(so, F32)] * 2,
+            out_shape=[vm(si, F32), vm(so, F32)] * 2,
             in_specs=[any_spec] * 4,
-            out_specs=[any_spec] * 4,
+            out_specs=[pl.BlockSpec(memory_space=pltpu.VMEM)] * 4,
             scratch_shapes=[
-                vm(si, F32), vm(so, F32), vm(si, F32), vm(so, F32),
                 vm(si, BF16), vm(so, BF16), vm(si, BF16), vm(so, BF16),
                 vm((2, 2, 3) + si, BF16), vm((2, 2, 3) + so, BF16), vm(si, BF16), vm(so, BF16),
                 vm(si, F32), vm(si, F32),
                 vm((2, rows, d), BF16), vm((2, rows, d), BF16), vm((layers - 1, rows, d), BF16),
                 vm((layers, rows, d), BF16), vm((layers, rows, d), F32), vm((layers, rows, ff), F32),
                 vm((layers, rows, ff), BF16), vm((rows, d), BF16),
-                sem((4,)), sem((2, 2)), sem((2, 3, 2 * layers)), sem((2, 2, 3, 2 * layers)),
+                sem((2,)), sem((2, 2)), sem((2, 3, 2 * layers)), sem((2, 2, 3, 2 * layers)),
             ],
-            compiler_params=pltpu.CompilerParams(collective_id=0, has_side_effects=True, vmem_limit_bytes=64000000),
+            compiler_params=pltpu.CompilerParams(collective_id=0, has_side_effects=True, vmem_limit_bytes=56000000),
         )(w_in[0, 0], w_out[0, 0], inputs[0, 0], targets[0, 0])
+        outs = pl.pallas_call(
+            flush,
+            out_shape=[jax.ShapeDtypeStruct(o.shape, o.dtype) for o in outs],
+            in_specs=[pl.BlockSpec(memory_space=pltpu.VMEM)] * 4,
+            out_specs=[any_spec] * 4,
+            scratch_shapes=[sem((4,))],
+        )(*[pltpu.with_memory_space_constraint(o, pltpu.VMEM) for o in outs])
         return tuple(o[None, None] for o in outs)
 
     block_spec = P('tx', 'ty')

time: 248 us -> 218 us (0.88)
  Pallas kernels: 242 us -> 218 us
  local copies, waits for them, and re-layouts: 6.01 us -> 0 us
    pallas_call x1, Pallas kernels: 242 us -> 216 us  [device_fn(): pl.pallas_call(functools.partial(kernel, (size_x, size_y, layers, steps))...]
    unnamed x8 -> x0, local copies, waits for them, and re-layouts: 6.01 us -> none
where the time goes in v2:
time: 218 us
  Pallas kernels  218 us (100%)
    pallas_call x1, Pallas kernels, device_fn(): pl.pallas_call(functools.partial(kernel, (size_x, size_y, layers, steps))...  216 us

profile of v2, /device:TPU:0, one launch (start us, length us, event | category | flops | bytes accessed | tf_op | source)
XLA Modules:
  0.0 218.3 jit_solution(1625203611027243963)
XLA Ops:
  0.6 215.9 %shard_map.75 = (f32[3,128,512]{2,1,0:T(8,128)S(1)}, f32[3,512,128]{2,1,0:T(8,128)S(1)}, f32[3,128,512]{2,1,0:T(8,128)S(1)}, f32[3,512,128]{2,1,0:T(8,128)S(1)}) custom-call(f32[3,128,512]{2,1,0:T(8,128)} %bitcast.10, f32[3,512,128]{2,1,0:T(8,128)} %bitcast.11, bf16[7,2048,128]{2,1,0:T(8,128)(2,1)} %bitcast.8, bf16[7,2048,128]{2,1,0:T(8,128)(2,1)} %bitcast.9), custom_call_target="tpu_custom_call" | custom-call | tf_op jit(solution)/shard_map/pallas_call | solution.py:217
  216.6 1.7 shard_map.76

commit v3 on v2

v3 whole, which is shorter than its diff:
```python
import functools

import jax
import jax.numpy as jnp
from jax import lax
from jax.experimental import pallas as pl
from jax.experimental.pallas import tpu as pltpu
from jax.sharding import PartitionSpec as P

EPS = 1e-6
LEARN_RATE = 0.125
F32 = jnp.float32
BF16 = jnp.bfloat16
C0 = 0.7978845608028654
C1 = 0.7978845608028654 * 0.044715
TILE = 1024
LINE = 4
MESH = pl.DeviceIdType.MESH


def dot(a, b, dims):
    return lax.dot_general(a, b, (dims, ((), ())), preferred_element_type=F32)


def forward_tile(rows, h_in, win, wout, u_ref, inv_ref, gp_ref, a_ref):
    d = h_in.shape[-1]
    hf = h_in[rows, :].astype(F32)
    ms = jnp.sum(hf * hf, axis=-1, keepdims=True) * (1.0 / d)
    inv = jnp.broadcast_to(lax.rsqrt(ms + EPS), hf.shape)
    inv_ref[rows, :] = inv
    u = (hf * inv).astype(BF16)
    u_ref[rows, :] = u
    z = dot(u, win[...], ((1,), (0,)))
    z2 = z * z
    t = jnp.tanh(z * (C0 + C1 * z2))
    w = 0.5 + 0.5 * t
    a = (z * w).astype(BF16)
    a_ref[rows, :] = a
    gp_ref[rows, :] = w + (w - w * w) * (z * (2.0 * C0 + (6.0 * C1) * z2))
    mlp = dot(a, wout[...], ((1,), (0,)))
    return (hf + mlp).astype(BF16)


def backward_tile(rows, first, h_in, win, wout, u_ref, inv_ref, gp_ref, a_ref, dh_ref, dwin, dwoutt):
    d = dh_ref[rows, :]
    da = dot(d, wout[...], ((1,), (1,))).astype(BF16).astype(F32)
    dz = (da * gp_ref[rows, :]).astype(BF16)
    dwoutt[...] += dot(d, a_ref[rows, :], ((0,), (0,)))
    dwin[...] += dot(u_ref[rows, :], dz, ((0,), (0,)))
    if not first:
        du = dot(dz, win[...], ((1,), (1,))).astype(BF16).astype(F32)
        hf = h_in[rows, :].astype(F32)
        inv = inv_ref[rows, :]
        s = jnp.sum(du * hf, axis=-1, keepdims=True) * (-1.0 / hf.shape[-1])
        dhf = d.astype(F32) + du * inv + hf * (inv * inv * inv * s)
        dh_ref[rows, :] = dhf.astype(BF16)


def kernel(dims, w_in, w_out, x_hbm, t_hbm, p_in, p_out, y_in, y_out,
           pb_in, pb_out, yb_in, yb_out, r_in, r_out, g_in, g_out,
           ps_in, ps_out, ys_in, ys_out, sp_in, sp_out, sy_in, sy_out,
           gb_in, gb_out, gs_in, gs_out, re_in, re_out, rp_in, rp_out,
           dw_in, dw_outt, xb, tb, hid, u_all, inv_all, gp_all, a_all, dh,
           lsem, xsem, ssem, rsem, esend, erecv, gsend, grecv, psend, precv, fsend, frecv):
    size_x, size_y, layers, steps = dims
    rows_n = xb.shape[1]
    me_x = lax.axis_index('tx')
    me_y = lax.axis_index('ty')
    pos = lax.rem(me_x, LINE)
    line = me_x - pos

    def along(off):
        return {'tx': lax.rem(me_x + size_x + off, size_x), 'ty': me_y}

    other = {'tx': me_x, 'ty': lax.rem(me_y + 1, size_y)}
    near = (along(1), along(-1), other)
    ends = (along(LINE), along(-LINE), other)
    mates = [{'tx': line + lax.rem(pos + k, LINE), 'ty': me_y} for k in range(1, LINE)]
    p_st, y_st, pb, yb, rcv, gold = (p_in, p_out), (y_in, y_out), (pb_in, pb_out), (yb_in, yb_out), (r_in, r_out), (g_in, g_out)
    ps, ys, sp, sy = (ps_in, ps_out), (ys_in, ys_out), (sp_in, sp_out), (sy_in, sy_out)
    gb, gs, redge, rpart = (gb_in, gb_out), (gs_in, gs_out), (re_in, re_out), (rp_in, rp_out)
    blk = tuple(ref.shape[1] // LINE for ref in ps)

    def block(k, b):
        return pl.ds(pl.multiple_of(b * blk[k], blk[k]), blk[k])

    def remote(src, dst, s, r, dev):
        return pltpu.make_async_remote_copy(src_ref=src, dst_ref=dst, send_sem=s, recv_sem=r, device_id=dev, device_id_type=MESH)

    def start(copies):
        for cp in copies:
            cp.start()

    def wait(copies):
        for cp in copies:
            cp.wait()

    def loads():
        return [pltpu.make_async_copy(w_in, p_in, lsem.at[0]), pltpu.make_async_copy(w_out, p_out, lsem.at[1])]

    def batch(t, slot):
        return [pltpu.make_async_copy(x_hbm.at[t], xb.at[slot], xsem.at[slot, 0]),
                pltpu.make_async_copy(t_hbm.at[t], tb.at[slot], xsem.at[slot, 1])]

    def bulk(kind, par):
        return [remote((pb[k].at[0], yb[k])[kind], rcv[k].at[kind, par, d], ssem.at[kind, d, k], rsem.at[kind, par, d, k], near[d])
                for k in range(2) for d in range(3)]

    def mix0(v, kind, par, k):
        s = v + rcv[k][kind, par, 0].astype(F32)
        s = s + rcv[k][kind, par, 1].astype(F32)
        n = rcv[k][kind, par, 2].astype(F32)
        return (s + n + n) * 0.2

    def edges(kind, par, lb):
        out = []
        for k in range(2):
            src = (sp, sy)[kind][k].at[par, lb]
            m = lb * 2 + k
            for d in range(3):
                part = (src.at[pl.ds((LINE - 1) * blk[k], blk[k])], src.at[pl.ds(0, blk[k])], src)[d]
                dst = redge[k].at[kind, par, d, lb] if d < 2 else rpart[k].at[kind, par, lb]
                out.append(remote(part, dst, esend.at[kind, d, m], erecv.at[kind, par, d, m], ends[d]))
        return out

    def swap(src, dst, send, recv, lb):
        out = []
        for k in range(2):
            for n, dev in enumerate(mates):
                out.append(remote(src[k].at[block(k, lax.rem(pos + n + 1, LINE))], dst[k].at[block(k, pos)],
                                  send.at[lb * 2 + k, n], recv.at[lb * 2 + k, n], dev))
        return out

    def g_swap(par, lb):
        return swap([g.at[par, lb] for g in gb], [g.at[par, lb] for g in gs], gsend, grecv, lb)

    def p_swap(par, lb):
        return swap([s.at[par, lb] for s in sp], [w.at[lb + 1] for w in pb], psend, precv, lb)

    def p_swap_f32(lb):
        return swap([s.at[lb] for s in ps], [w.at[lb + 1] for w in p_st], psend, precv, lb)

    def y_swap_f32(lb):
        return swap([s.at[lb] for s in ys], [w.at[lb + 1] for w in y_st], fsend, frecv, lb)

    def first_swap(lb):
        return swap([w.at[lb + 1] for w in p_st], [s.at[lb] for s in ps], fsend, frecv, lb)

    def mix_b(v, kind, par, lb, k, b):
        src = (sp, sy)[kind][k]
        rows = slice(b * blk[k], (b + 1) * blk[k])
        lo = redge[k][kind, par, 0, lb] if b == 0 else src[par, lb, (b - 1) * blk[k]:b * blk[k], :]
        hi = redge[k][kind, par, 1, lb] if b == LINE - 1 else src[par, lb, (b + 1) * blk[k]:(b + 2) * blk[k], :]
        n = rpart[k][kind, par, lb, rows, :].astype(F32)
        return (v + lo.astype(F32) + hi.astype(F32) + n + n) * 0.2

    def own_rows(lb, t, slot, nxt):
        wait(g_swap(nxt, lb))
        wait(edges(0, nxt, lb))

        @pl.when(t >= 2)
        def _():
            wait(edges(1, slot, lb))

        for k in range(2):
            for b in range(LINE):
                rows = slice(b * blk[k], (b + 1) * blk[k])
                g = gs[k][nxt, lb, rows, :].astype(F32)

                @pl.when(t == 1)
                def _():
                    ys[k][lb, rows, :] = g

                @pl.when(t >= 2)
                def _():
                    ys[k][lb, rows, :] = (mix_b(ys[k][lb, rows, :], 1, slot, lb, k, b) + g) - gs[k][slot, lb, rows, :].astype(F32)

                y = ys[k][lb, rows, :]
                p = mix_b(ps[k][lb, rows, :], 0, nxt, lb, k, b) - LEARN_RATE * y
                ps[k][lb, rows, :] = p
                sp[k][slot, lb, rows, :] = p.astype(BF16)
                sy[k][nxt, lb, rows, :] = y.astype(BF16)

        @pl.when(t < steps)
        def _():
            for k in range(2):
                pb[k][lb + 1, block(k, pos), :] = sp[k][slot, lb, block(k, pos), :]
            start(p_swap(slot, lb))
            start(edges(0, slot, lb))

        @pl.when(t == steps)
        def _():
            for k in range(2):
                p_st[k][lb + 1, block(k, pos), :] = ps[k][lb, block(k, pos), :]
            start(p_swap_f32(lb))

        start(edges(1, nxt, lb))

    def last_trackers(lb, par):
        wait(edges(1, par, lb))
        for k in range(2):
            for b in range(LINE):
                rows = slice(b * blk[k], (b + 1) * blk[k])
                ys[k][lb, rows, :] = mix_b(ys[k][lb, rows, :], 1, par, lb, k, b)
            y_st[k][lb + 1, block(k, pos), :] = ys[k][lb, block(k, pos), :]
        start(y_swap_f32(lb))

    def take_weights(lb, t, slot):
        @pl.when(jnp.logical_and(t >= 1, t < steps))
        def _():
            wait(p_swap(slot, lb))

        @pl.when(t == steps)
        def _():
            wait(p_swap_f32(lb))
            for k in range(2):
                pb[k][lb + 1] = p_st[k][lb + 1].astype(BF16)

    start(loads() + batch(0, 0))
    barrier = pltpu.get_barrier_semaphore()
    for peer in mates + list(near) + list(ends[:2]):
        pl.semaphore_signal(barrier, inc=1, device_id=peer, device_id_type=MESH)
    wait(loads())
    pl.semaphore_wait(barrier, LINE + 4)
    for lb in range(layers - 1):
        start(first_swap(lb))
    for k in range(2):
        for l in range(layers):
            pb[k][l] = p_st[k][l].astype(BF16)
        for lb in range(layers - 1):
            ps[k][lb, block(k, pos), :] = p_st[k][lb + 1, block(k, pos), :]
    start(bulk(0, 0))

    def step(t, carry):
        slot = lax.rem(t, 2)
        nxt = 1 - slot
        tiles = rows_n // TILE
        wait(batch(t, slot))

        @pl.when(t < steps)
        def _():
            start(batch(t + 1, nxt))

        def fwd(i, l, h_in):
            rows = pl.ds(pl.multiple_of(i * TILE, TILE), TILE)
            h = forward_tile(rows, h_in, pb_in.at[l], pb_out.at[l], u_all.at[l], inv_all.at[l], gp_all.at[l], a_all.at[l])
            if l + 1 < layers:
                hid[l, rows, :] = h
            else:
                err = h.astype(F32) - tb[slot, rows, :].astype(F32)
                dh[rows, :] = (err * (2.0 / (rows_n * h.shape[-1]))).astype(BF16)

        def bwd(i, l, h_in):
            rows = pl.ds(pl.multiple_of(i * TILE, TILE), TILE)
            backward_tile(rows, l == 0, h_in, pb_in.at[l], pb_out.at[l], u_all.at[l], inv_all.at[l], gp_all.at[l],
                          a_all.at[l], dh, dw_in.at[l], dw_outt.at[l])

        for l in range(layers):
            h_in = xb.at[slot] if l == 0 else hid.at[l - 1]
            if l > 0:
                take_weights(l - 1, t, slot)

            def body(i, c, l=l, h_in=h_in):
                fwd(i, l, h_in)
                if l == 0:
                    @pl.when(jnp.logical_and(t >= 1, i == 0))
                    def _():
                        own_rows(1, t, slot, nxt)

                    @pl.when(jnp.logical_and(t >= 1, i == tiles - 1))
                    def _():
                        own_rows(0, t, slot, nxt)
                        start(bulk(1, nxt))
                return c

            lax.fori_loop(0, tiles, body, 0)
            if l == 0:
                @pl.when(jnp.logical_and(t >= 1, t < steps))
                def _():
                    start(bulk(0, slot))

                @pl.when(t == steps)
                def _():
                    for lb in reversed(range(layers - 1)):
                        last_trackers(lb, nxt)

        for l in reversed(range(layers)):
            h_in = xb.at[slot] if l == 0 else hid.at[l - 1]
            dw_in[l] = jnp.zeros_like(dw_in[l])
            dw_outt[l] = jnp.zeros_like(dw_outt[l])

            def body(i, c, l=l, h_in=h_in):
                bwd(i, l, h_in)
                return c

            lax.fori_loop(0, tiles, body, 0)
            if l > 0:
                gb_in[slot, l - 1] = dw_in[l].astype(BF16)
                gb_out[slot, l - 1] = dw_outt[l].T.astype(BF16)

                @pl.when(t < steps)
                def _():
                    for k in range(2):
                        gs[k][slot, l - 1, block(k, pos), :] = gb[k][slot, l - 1, block(k, pos), :]
                    start(g_swap(slot, l - 1))
            if l == 1:
                @pl.when(t == 0)
                def _():
                    for lb in reversed(range(layers - 1)):
                        wait(first_swap(lb))
                        for k in range(2):
                            sp[k][0, lb] = ps[k][lb].astype(BF16)
                        start(edges(0, 0, lb))

        @pl.when(t > 0)
        def _():
            wait(bulk(1, nxt))

        for k in range(2):
            g = (dw_in[0] if k == 0 else dw_outt[0].T).astype(BF16).astype(F32)

            @pl.when(t == 0)
            def _():
                y_st[k][0] = g

            @pl.when(t > 0)
            def _():
                y_st[k][0] = (mix0(y_st[k][0], 1, nxt, k) + g) - gold[k][...].astype(F32)

            gold[k][...] = g.astype(BF16)

        @pl.when(t < steps)
        def _():
            wait(bulk(0, slot))
            for k in range(2):
                y = y_st[k][0]
                yb[k][...] = y.astype(BF16)
                p = mix0(p_st[k][0], 0, slot, k) - LEARN_RATE * y
                p_st[k][0] = p
                pb[k][0] = p.astype(BF16)
        return carry

    lax.fori_loop(0, steps + 1, step, 0)
    new, old = steps % 2, (steps - 1) % 2
    for lb in reversed(range(layers - 1)):
        wait(y_swap_f32(lb))
        for k in range(2):
            y_st[k][lb + 1] = (y_st[k][lb + 1] + gb[k][new, lb].astype(F32)) - gb[k][old, lb].astype(F32)


def flush(*refs):
    copies = [pltpu.make_async_copy(refs[n], refs[4 + n], refs[8].at[n]) for n in range(4)]
    for cp in copies:
        cp.start()
    for cp in copies:
        cp.wait()


def solution(mesh):
    size_x = mesh.shape['tx']
    size_y = mesh.shape['ty']

    def device_fn(w_in, w_out, inputs, targets):
        _, _, layers, d, ff = w_in.shape
        steps = inputs.shape[2] - 1
        rows = inputs.shape[3]
        si, so = (d, ff), (ff, d)
        ei, eo = (d // LINE, ff), (ff // LINE, d)
        nb = layers - 1
        vm = pltpu.VMEM
        sem = pltpu.SemaphoreType.DMA
        any_spec = pl.BlockSpec(memory_space=pl.ANY)

        def both(lead, dtype):
            return [vm(lead + si, dtype), vm(lead + so, dtype)]

        outs = pl.pallas_call(
            functools.partial(kernel, (size_x, size_y, layers, steps)),
            out_shape=both((layers,), F32) * 2,
            in_specs=[any_spec] * 4,
            out_specs=[pl.BlockSpec(memory_space=pltpu.VMEM)] * 4,
            scratch_shapes=both((layers,), BF16) + both((), BF16) + both((2, 2, 3), BF16) + both((), BF16)
            + both((nb,), F32) * 2 + both((2, nb), BF16) * 4
            + [vm((2, 2, 2, nb) + ei, BF16), vm((2, 2, 2, nb) + eo, BF16)] + both((2, 2, nb), BF16)
            + [vm((layers,) + si, F32), vm((layers,) + si, F32),
               vm((2, rows, d), BF16), vm((2, rows, d), BF16), vm((layers - 1, rows, d), BF16),
               vm((layers, rows, d), BF16), vm((layers, rows, d), F32), vm((layers, rows, ff), F32),
               vm((layers, rows, ff), BF16), vm((rows, d), BF16),
               sem((2,)), sem((2, 2)), sem((2, 3, 2)), sem((2, 2, 3, 2)),
               sem((2, 3, 2 * nb)), sem((2, 2, 3, 2 * nb)),
               sem((2 * nb, 3)), sem((2 * nb, 3)), sem((2 * nb, 3)), sem((2 * nb, 3)), sem((2 * nb, 3)), sem((2 * nb, 3))],
            compiler_params=pltpu.CompilerParams(collective_id=0, has_side_effects=True, vmem_limit_bytes=56000000),
        )(w_in[0, 0], w_out[0, 0], inputs[0, 0], targets[0, 0])
        outs = pl.pallas_call(
            flush,
            out_shape=[jax.ShapeDtypeStruct(o.shape, o.dtype) for o in outs],
            in_specs=[pl.BlockSpec(memory_space=pltpu.VMEM)] * 4,
            out_specs=[any_spec] * 4,
            scratch_shapes=[sem((4,))],
        )(*[pltpu.with_memory_space_constraint(o, pltpu.VMEM) for o in outs])
        return tuple(o[None, None] for o in outs)

    block_spec = P('tx', 'ty')
    return jax.shard_map(device_fn, mesh=mesh, in_specs=(block_spec,) * 4, out_specs=(block_spec,) * 4, check_vma=False)
```

time: 218 us -> 189 us (0.87)
  Pallas kernels: 218 us -> 188 us
    pallas_call x1, Pallas kernels: 216 us -> 187 us  [device_fn(): pl.pallas_call(functools.partial(kernel, (size_x, size_y, layers, steps))...]
where the time goes in v3:
time: 189 us
  Pallas kernels  188 us (99%)
    pallas_call x1, Pallas kernels, device_fn(): pl.pallas_call(functools.partial(kernel, (size_x, size_y, layers, steps))...  187 us

profile of v3, /device:TPU:0, one launch (start us, length us, event | category | flops | bytes accessed | tf_op | source)
XLA Modules:
  0.0 189.1 jit_solution(8161734161628463705)
XLA Ops:
  0.6 186.8 %shard_map.75 = (f32[3,128,512]{2,1,0:T(8,128)S(1)}, f32[3,512,128]{2,1,0:T(8,128)S(1)}, f32[3,128,512]{2,1,0:T(8,128)S(1)}, f32[3,512,128]{2,1,0:T(8,128)S(1)}) custom-call(f32[3,128,512]{2,1,0:T(8,128)} %bitcast.10, f32[3,512,128]{2,1,0:T(8,128)} %bitcast.11, bf16[7,2048,128]{2,1,0:T(8,128)(2,1)} %bitcast.8, bf16[7,2048,128]{2,1,0:T(8,128)(2,1)} %bitcast.9), custom_call_target="tpu_custom_call" | custom-call | tf_op jit(solution)/shard_map/pallas_call | solution.py:377
  187.4 1.7 shard_map.76

commit v4 on v3

--- a/solution.py
+++ b/solution.py
@@ -22,7 +22,11 @@
     return lax.dot_general(a, b, (dims, ((), ())), preferred_element_type=F32)
 
 
-def forward_tile(rows, h_in, win, wout, u_ref, inv_ref, gp_ref, a_ref):
+def gelu_weight(z, z2):
+    return 0.5 + 0.5 * jnp.tanh(z * (C0 + C1 * z2))
+
+
+def forward_tile(rows, h_in, win, wout, u_ref, inv_ref, z_ref, w_ref, a_ref, before_out=None):
     d = h_in.shape[-1]
     hf = h_in[rows, :].astype(F32)
     ms = jnp.sum(hf * hf, axis=-1, keepdims=True) * (1.0 / d)
@@ -31,21 +35,27 @@
     u = (hf * inv).astype(BF16)
     u_ref[rows, :] = u
     z = dot(u, win[...], ((1,), (0,)))
-    z2 = z * z
-    t = jnp.tanh(z * (C0 + C1 * z2))
-    w = 0.5 + 0.5 * t
+    z_ref[rows, :] = z
+    w = gelu_weight(z, z * z)
+    w_ref[rows, :] = w
     a = (z * w).astype(BF16)
     a_ref[rows, :] = a
-    gp_ref[rows, :] = w + (w - w * w) * (z * (2.0 * C0 + (6.0 * C1) * z2))
+    if before_out is not None:
+        before_out()
     mlp = dot(a, wout[...], ((1,), (0,)))
     return (hf + mlp).astype(BF16)
 
 
-def backward_tile(rows, first, h_in, win, wout, u_ref, inv_ref, gp_ref, a_ref, dh_ref, dwin, dwoutt):
+def backward_tile(rows, first, h_in, win, wout, u_ref, inv_ref, z_ref, w_ref, a_ref, dh_ref, dwin, dwoutt):
     d = dh_ref[rows, :]
     da = dot(d, wout[...], ((1,), (1,))).astype(BF16).astype(F32)
-    dz = (da * gp_ref[rows, :]).astype(BF16)
-    dwoutt[...] += dot(d, a_ref[rows, :], ((0,), (0,)))
+    z = z_ref[rows, :]
+    z2 = z * z
+    w = w_ref[rows, :]
+    gp = w + (w - w * w) * (z * (2.0 * C0 + (6.0 * C1) * z2))
+    dz = (da * gp).astype(BF16)
+    a = a_ref[rows, :]
+    dwoutt[...] += dot(d, a, ((0,), (0,)))
     dwin[...] += dot(u_ref[rows, :], dz, ((0,), (0,)))
     if not first:
         du = dot(dz, win[...], ((1,), (1,))).astype(BF16).astype(F32)
@@ -60,7 +70,7 @@
            pb_in, pb_out, yb_in, yb_out, r_in, r_out, g_in, g_out,
            ps_in, ps_out, ys_in, ys_out, sp_in, sp_out, sy_in, sy_out,
            gb_in, gb_out, gs_in, gs_out, re_in, re_out, rp_in, rp_out,
-           dw_in, dw_outt, xb, tb, hid, u_all, inv_all, gp_all, a_all, dh,
+           dw_in, dw_outt, xb, tb, hid, u_all, inv_all, z_all, w_all, a_all, dh,
            lsem, xsem, ssem, rsem, esend, erecv, gsend, grecv, psend, precv, fsend, frecv):
     size_x, size_y, layers, steps = dims
     rows_n = xb.shape[1]
@@ -112,9 +122,9 @@
         n = rcv[k][kind, par, 2].astype(F32)
         return (s + n + n) * 0.2
 
-    def edges(kind, par, lb):
+    def edges(kind, par, lb, ks=(0, 1)):
         out = []
-        for k in range(2):
+        for k in ks:
             src = (sp, sy)[kind][k].at[par, lb]
             m = lb * 2 + k
             for d in range(3):
@@ -123,28 +133,28 @@
                 out.append(remote(part, dst, esend.at[kind, d, m], erecv.at[kind, par, d, m], ends[d]))
         return out
 
-    def swap(src, dst, send, recv, lb):
+    def swap(src, dst, send, recv, lb, ks=(0, 1)):
         out = []
-        for k in range(2):
+        for k in ks:
             for n, dev in enumerate(mates):
                 out.append(remote(src[k].at[block(k, lax.rem(pos + n + 1, LINE))], dst[k].at[block(k, pos)],
                                   send.at[lb * 2 + k, n], recv.at[lb * 2 + k, n], dev))
         return out
 
-    def g_swap(par, lb):
-        return swap([g.at[par, lb] for g in gb], [g.at[par, lb] for g in gs], gsend, grecv, lb)
-
-    def p_swap(par, lb):
-        return swap([s.at[par, lb] for s in sp], [w.at[lb + 1] for w in pb], psend, precv, lb)
-
-    def p_swap_f32(lb):
-        return swap([s.at[lb] for s in ps], [w.at[lb + 1] for w in p_st], psend, precv, lb)
+    def g_swap(par, lb, ks=(0, 1)):
+        return swap([g.at[par, lb] for g in gb], [g.at[par, lb] for g in gs], gsend, grecv, lb, ks)
+
+    def p_swap(par, lb, ks=(0, 1)):
+        return swap([s.at[par, lb] for s in sp], [w.at[lb + 1] for w in pb], psend, precv, lb, ks)
+
+    def p_swap_f32(lb, ks=(0, 1)):
+        return swap([s.at[lb] for s in ps], [w.at[lb + 1] for w in p_st], psend, precv, lb, ks)
 
     def y_swap_f32(lb):
         return swap([s.at[lb] for s in ys], [w.at[lb + 1] for w in y_st], fsend, frecv, lb)
 
     def first_swap(lb):
-        return swap([w.at[lb + 1] for w in p_st], [s.at[lb] for s in ps], fsend, frecv, lb)
+        return swap([w.at[lb + 1] for w in (w_in, w_out)], [s.at[lb] for s in ps], fsend, frecv, lb)
 
     def mix_b(v, kind, par, lb, k, b):
         src = (sp, sy)[kind][k]
@@ -155,7 +165,6 @@
         return (v + lo.astype(F32) + hi.astype(F32) + n + n) * 0.2
 
     def own_rows(lb, t, slot, nxt):
-        wait(g_swap(nxt, lb))
         wait(edges(0, nxt, lb))
 
         @pl.when(t >= 2)
@@ -163,36 +172,40 @@
             wait(edges(1, slot, lb))
 
         for k in range(2):
+            wait(g_swap(nxt, lb, (k,)))
+
+            @pl.when(t == 1)
+            def _():
+                ys[k][lb] = gs[k][nxt, lb].astype(F32)
+
+            @pl.when(t >= 2)
+            def _():
+                for b in range(LINE):
+                    rows = slice(b * blk[k], (b + 1) * blk[k])
+                    g = gs[k][nxt, lb, rows, :].astype(F32)
+                    ys[k][lb, rows, :] = (mix_b(ys[k][lb, rows, :], 1, slot, lb, k, b) + g) - gs[k][slot, lb, rows, :].astype(F32)
+
             for b in range(LINE):
                 rows = slice(b * blk[k], (b + 1) * blk[k])
-                g = gs[k][nxt, lb, rows, :].astype(F32)
-
-                @pl.when(t == 1)
-                def _():
-                    ys[k][lb, rows, :] = g
-
-                @pl.when(t >= 2)
-                def _():
-                    ys[k][lb, rows, :] = (mix_b(ys[k][lb, rows, :], 1, slot, lb, k, b) + g) - gs[k][slot, lb, rows, :].astype(F32)
-
                 y = ys[k][lb, rows, :]
                 p = mix_b(ps[k][lb, rows, :], 0, nxt, lb, k, b) - LEARN_RATE * y
                 ps[k][lb, rows, :] = p
                 sp[k][slot, lb, rows, :] = p.astype(BF16)
                 sy[k][nxt, lb, rows, :] = y.astype(BF16)
 
+            @pl.when(t < steps)
+            def _():
+                pb[k][lb + 1, block(k, pos), :] = sp[k][slot, lb, block(k, pos), :]
+                start(p_swap(slot, lb, (k,)))
+
+            @pl.when(t == steps)
+            def _():
+                p_st[k][lb + 1, block(k, pos), :] = ps[k][lb, block(k, pos), :]
+                start(p_swap_f32(lb, (k,)))
+
         @pl.when(t < steps)
         def _():
-            for k in range(2):
-                pb[k][lb + 1, block(k, pos), :] = sp[k][slot, lb, block(k, pos), :]
-            start(p_swap(slot, lb))
             start(edges(0, slot, lb))
-
-        @pl.when(t == steps)
-        def _():
-            for k in range(2):
-                p_st[k][lb + 1, block(k, pos), :] = ps[k][lb, block(k, pos), :]
-            start(p_swap_f32(lb))
 
         start(edges(1, nxt, lb))
 
@@ -205,25 +218,25 @@
             y_st[k][lb + 1, block(k, pos), :] = ys[k][lb, block(k, pos), :]
         start(y_swap_f32(lb))
 
-    def take_weights(lb, t, slot):
+    def take_weights(lb, t, slot, ks):
         @pl.when(jnp.logical_and(t >= 1, t < steps))
         def _():
-            wait(p_swap(slot, lb))
+            wait(p_swap(slot, lb, ks))
 
         @pl.when(t == steps)
         def _():
-            wait(p_swap_f32(lb))
-            for k in range(2):
+            wait(p_swap_f32(lb, ks))
+            for k in ks:
                 pb[k][lb + 1] = p_st[k][lb + 1].astype(BF16)
 
-    start(loads() + batch(0, 0))
     barrier = pltpu.get_barrier_semaphore()
     for peer in mates + list(near) + list(ends[:2]):
         pl.semaphore_signal(barrier, inc=1, device_id=peer, device_id_type=MESH)
-    wait(loads())
+    start(loads() + batch(0, 0))
     pl.semaphore_wait(barrier, LINE + 4)
     for lb in range(layers - 1):
         start(first_swap(lb))
+    wait(loads())
     for k in range(2):
         for l in range(layers):
             pb[k][l] = p_st[k][l].astype(BF16)
@@ -241,9 +254,9 @@
         def _():
             start(batch(t + 1, nxt))
 
-        def fwd(i, l, h_in):
-            rows = pl.ds(pl.multiple_of(i * TILE, TILE), TILE)
-            h = forward_tile(rows, h_in, pb_in.at[l], pb_out.at[l], u_all.at[l], inv_all.at[l], gp_all.at[l], a_all.at[l])
+        def fwd(i, l, h_in, before_out=None):
+            rows = pl.ds(i * TILE if isinstance(i, int) else pl.multiple_of(i * TILE, TILE), TILE)
+            h = forward_tile(rows, h_in, pb_in.at[l], pb_out.at[l], u_all.at[l], inv_all.at[l], z_all.at[l], w_all.at[l], a_all.at[l], before_out)
             if l + 1 < layers:
                 hid[l, rows, :] = h
             else:
@@ -252,13 +265,13 @@
 
         def bwd(i, l, h_in):
             rows = pl.ds(pl.multiple_of(i * TILE, TILE), TILE)
-            backward_tile(rows, l == 0, h_in, pb_in.at[l], pb_out.at[l], u_all.at[l], inv_all.at[l], gp_all.at[l],
+            backward_tile(rows, l == 0, h_in, pb_in.at[l], pb_out.at[l], u_all.at[l], inv_all.at[l], z_all.at[l], w_all.at[l],
                           a_all.at[l], dh, dw_in.at[l], dw_outt.at[l])
 
         for l in range(layers):
             h_in = xb.at[slot] if l == 0 else hid.at[l - 1]
             if l > 0:
-                take_weights(l - 1, t, slot)
+                take_weights(l - 1, t, slot, (0,) if l == 1 else (0, 1))
 
             def body(i, c, l=l, h_in=h_in):
                 fwd(i, l, h_in)
@@ -273,7 +286,9 @@
                         start(bulk(1, nxt))
                 return c
 
-            lax.fori_loop(0, tiles, body, 0)
+            if l == 1:
+                fwd(0, l, h_in, lambda: take_weights(0, t, slot, (1,)))
+            lax.fori_loop(1 if l == 1 else 0, tiles, body, 0)
             if l == 0:
                 @pl.when(jnp.logical_and(t >= 1, t < steps))
                 def _():
@@ -385,11 +400,11 @@
             + [vm((layers,) + si, F32), vm((layers,) + si, F32),
                vm((2, rows, d), BF16), vm((2, rows, d), BF16), vm((layers - 1, rows, d), BF16),
                vm((layers, rows, d), BF16), vm((layers, rows, d), F32), vm((layers, rows, ff), F32),
-               vm((layers, rows, ff), BF16), vm((rows, d), BF16),
+               vm((layers, rows, ff), F32), vm((layers, rows, ff), BF16), vm((rows, d), BF16),
                sem((2,)), sem((2, 2)), sem((2, 3, 2)), sem((2, 2, 3, 2)),
                sem((2, 3, 2 * nb)), sem((2, 2, 3, 2 * nb)),
                sem((2 * nb, 3)), sem((2 * nb, 3)), sem((2 * nb, 3)), sem((2 * nb, 3)), sem((2 * nb, 3)), sem((2 * nb, 3))],
-            compiler_params=pltpu.CompilerParams(collective_id=0, has_side_effects=True, vmem_limit_bytes=56000000),
+            compiler_params=pltpu.CompilerParams(collective_id=0, has_side_effects=True, vmem_limit_bytes=62000000),
         )(w_in[0, 0], w_out[0, 0], inputs[0, 0], targets[0, 0])
         outs = pl.pallas_call(
             flush,

time: 189 us -> 186 us (0.984)
  Pallas kernels: 188 us -> 179 us
  local copies, waits for them, and re-layouts: 0 us -> 6.03 us
    pallas_call x1, Pallas kernels: 187 us -> 177 us  [device_fn(): pl.pallas_call(functools.partial(kernel, (size_x, size_y, layers, steps))...]
    unnamed x0 -> x12, local copies, waits for them, and re-layouts: none -> 6.03 us
where the time goes in v4:
time: 186 us; the launch traced here: 185 us
  Pallas kernels  179 us (96%)
  local copies, waits for them, and re-layouts  6.03 us (3%)
    pallas_call x1, Pallas kernels, device_fn(): pl.pallas_call(functools.partial(kernel, (size_x, size_y, layers, steps))...  177 us
    unnamed x12, local copies, waits for them, and re-layouts  6.03 us

profile of v4, /device:TPU:0, one launch (start us, length us, event | category | flops | bytes accessed | tf_op | source)
XLA Modules:
  0.0 185.4 jit_solution(18141375505399909990)
XLA Ops:
  0.6 177.1 %shard_map.75 = (f32[3,128,512]{2,1,0:T(8,128)S(1)}, f32[3,512,128]{2,1,0:T(8,128)S(1)}, f32[3,128,512]{2,1,0:T(8,128)S(1)}, f32[3,512,128]{2,1,0:T(8,128)S(1)}) custom-call(f32[3,128,512]{2,1,0:T(8,128)} %bitcast.10, f32[3,512,128]{2,1,0:T(8,128)} %bitcast.11, bf16[7,2048,128]{2,1,0:T(8,128)(2,1)} %bitcast.8, bf16[7,2048,128]{2,1,0:T(8,128)(2,1)} %bitcast.9), custom_call_target="tpu_custom_call" | custom-call | tf_op jit(solution)/shard_map/pallas_call | solution.py:392
  177.7 0.0 copy-start
  177.7 0.9 copy-done
  178.6 0.0 copy-start.2
  178.6 0.9 copy-done.2
  179.5 0.0 copy-start.4
  179.5 0.9 copy-done.4
  180.3 0.0 copy-start.1
  180.3 1.1 copy-done.1
  181.5 0.0 copy-start.3
  181.5 1.1 copy-done.3
  182.6 0.0 copy-start.5
  182.6 1.1 copy-done.5
  183.7 1.7 shard_map.76
Async XLA Ops:
  177.7 0.9 copy-start
  178.6 0.9 copy-start.2
  179.5 0.9 copy-start.4
  180.3 1.1 copy-start.1
  181.5 1.1 copy-start.3
  182.6 1.1 copy-start.5

commit v5 on v4

--- a/solution.py
+++ b/solution.py
@@ -26,14 +26,19 @@
     return 0.5 + 0.5 * jnp.tanh(z * (C0 + C1 * z2))
 
 
+def normed(hf):
+    ms = jnp.sum(hf * hf, axis=-1, keepdims=True) * (1.0 / hf.shape[-1])
+    inv = jnp.broadcast_to(lax.rsqrt(ms + EPS), hf.shape)
+    return inv, (hf * inv).astype(BF16)
+
+
 def forward_tile(rows, h_in, win, wout, u_ref, inv_ref, z_ref, w_ref, a_ref, before_out=None):
-    d = h_in.shape[-1]
     hf = h_in[rows, :].astype(F32)
-    ms = jnp.sum(hf * hf, axis=-1, keepdims=True) * (1.0 / d)
-    inv = jnp.broadcast_to(lax.rsqrt(ms + EPS), hf.shape)
-    inv_ref[rows, :] = inv
-    u = (hf * inv).astype(BF16)
-    u_ref[rows, :] = u
+    if inv_ref is None:
+        u = u_ref[rows, :]
+    else:
+        inv_ref[rows, :], u = normed(hf)
+        u_ref[rows, :] = u
     z = dot(u, win[...], ((1,), (0,)))
     z_ref[rows, :] = z
     w = gelu_weight(z, z * z)
@@ -70,7 +75,7 @@
            pb_in, pb_out, yb_in, yb_out, r_in, r_out, g_in, g_out,
            ps_in, ps_out, ys_in, ys_out, sp_in, sp_out, sy_in, sy_out,
            gb_in, gb_out, gs_in, gs_out, re_in, re_out, rp_in, rp_out,
-           dw_in, dw_outt, xb, tb, hid, u_all, inv_all, z_all, w_all, a_all, dh,
+           dw_in, dw_outt, xb, tb, hid, u_first, u_all, inv_all, z_all, w_all, a_all, dh,
            lsem, xsem, ssem, rsem, esend, erecv, gsend, grecv, psend, precv, fsend, frecv):
     size_x, size_y, layers, steps = dims
     rows_n = xb.shape[1]
@@ -244,19 +249,33 @@
             ps[k][lb, block(k, pos), :] = p_st[k][lb + 1, block(k, pos), :]
     start(bulk(0, 0))
 
+    tiles = rows_n // TILE
+
+    def prepare(t, slot):
+        wait(batch(t, slot))
+
+        def body(i, c):
+            rows = pl.ds(pl.multiple_of(i * TILE, TILE), TILE)
+            u_first[slot, rows, :] = normed(xb[slot, rows, :].astype(F32))[1]
+            return c
+
+        lax.fori_loop(0, tiles, body, 0)
+
+    prepare(0, 0)
+
     def step(t, carry):
         slot = lax.rem(t, 2)
         nxt = 1 - slot
-        tiles = rows_n // TILE
-        wait(batch(t, slot))
-
         @pl.when(t < steps)
         def _():
             start(batch(t + 1, nxt))
+
+        def acts(l):
+            return (u_first.at[slot], None) if l == 0 else (u_all.at[l - 1], inv_all.at[l - 1])
 
         def fwd(i, l, h_in, before_out=None):
             rows = pl.ds(i * TILE if isinstance(i, int) else pl.multiple_of(i * TILE, TILE), TILE)
-            h = forward_tile(rows, h_in, pb_in.at[l], pb_out.at[l], u_all.at[l], inv_all.at[l], z_all.at[l], w_all.at[l], a_all.at[l], before_out)
+            h = forward_tile(rows, h_in, pb_in.at[l], pb_out.at[l], *acts(l), z_all.at[l], w_all.at[l], a_all.at[l], before_out)
             if l + 1 < layers:
                 hid[l, rows, :] = h
             else:
@@ -265,11 +284,19 @@
 
         def bwd(i, l, h_in):
             rows = pl.ds(pl.multiple_of(i * TILE, TILE), TILE)
-            backward_tile(rows, l == 0, h_in, pb_in.at[l], pb_out.at[l], u_all.at[l], inv_all.at[l], z_all.at[l], w_all.at[l],
+            backward_tile(rows, l == 0, h_in, pb_in.at[l], pb_out.at[l], *acts(l), z_all.at[l], w_all.at[l],
                           a_all.at[l], dh, dw_in.at[l], dw_outt.at[l])
 
         for l in range(layers):
             h_in = xb.at[slot] if l == 0 else hid.at[l - 1]
+            if l == 1:
+                dw_in[...] = jnp.zeros_like(dw_in)
+                dw_outt[...] = jnp.zeros_like(dw_outt)
+
+                @pl.when(t < steps)
+                def _():
+                    prepare(t + 1, nxt)
+
             if l > 0:
                 take_weights(l - 1, t, slot, (0,) if l == 1 else (0, 1))
 
@@ -301,9 +328,6 @@
 
         for l in reversed(range(layers)):
             h_in = xb.at[slot] if l == 0 else hid.at[l - 1]
-            dw_in[l] = jnp.zeros_like(dw_in[l])
-            dw_outt[l] = jnp.zeros_like(dw_outt[l])
-
             def body(i, c, l=l, h_in=h_in):
                 bwd(i, l, h_in)
                 return c
@@ -399,7 +423,7 @@
             + [vm((2, 2, 2, nb) + ei, BF16), vm((2, 2, 2, nb) + eo, BF16)] + both((2, 2, nb), BF16)
             + [vm((layers,) + si, F32), vm((layers,) + si, F32),
                vm((2, rows, d), BF16), vm((2, rows, d), BF16), vm((layers - 1, rows, d), BF16),
-               vm((layers, rows, d), BF16), vm((layers, rows, d), F32), vm((layers, rows, ff), F32),
+               vm((2, rows, d), BF16), vm((layers - 1, rows, d), BF16), vm((layers - 1, rows, d), F32), vm((layers, rows, ff), F32),
                vm((layers, rows, ff), F32), vm((layers, rows, ff), BF16), vm((rows, d), BF16),
                sem((2,)), sem((2, 2)), sem((2, 3, 2)), sem((2, 2, 3, 2)),
                sem((2, 3, 2 * nb)), sem((2, 2, 3, 2 * nb)),

time: 186 us -> 185 us (level)
  no operation moved by 1% of the time
where the time goes in v5:
time: 185 us
  Pallas kernels  178 us (96%)
  local copies, waits for them, and re-layouts  6.03 us (3%)
    pallas_call x1, Pallas kernels, device_fn(): pl.pallas_call(functools.partial(kernel, (size_x, size_y, layers, steps))...  176 us
    unnamed x12, local copies, waits for them, and re-layouts  6.03 us

profile of v5, /device:TPU:0, one launch (start us, length us, event | category | flops | bytes accessed | tf_op | source)
XLA Modules:
  0.0 184.5 jit_solution(17209976744321930173)
XLA Ops:
  0.6 176.1 %shard_map.75 = (f32[3,128,512]{2,1,0:T(8,128)S(1)}, f32[3,512,128]{2,1,0:T(8,128)S(1)}, f32[3,128,512]{2,1,0:T(8,128)S(1)}, f32[3,512,128]{2,1,0:T(8,128)S(1)}) custom-call(f32[3,128,512]{2,1,0:T(8,128)} %bitcast.10, f32[3,512,128]{2,1,0:T(8,128)} %bitcast.11, bf16[7,2048,128]{2,1,0:T(8,128)(2,1)} %bitcast.8, bf16[7,2048,128]{2,1,0:T(8,128)(2,1)} %bitcast.9), custom_call_target="tpu_custom_call" | custom-call | tf_op jit(solution)/shard_map/pallas_call | solution.py:416
  176.8 0.0 copy-start
  176.8 0.9 copy-done
  177.7 0.0 copy-start.2
  177.7 0.9 copy-done.2
  178.5 0.0 copy-start.4
  178.5 0.9 copy-done.4
  179.4 0.0 copy-start.1
  179.4 1.1 copy-done.1
  180.5 0.0 copy-start.3
  180.5 1.1 copy-done.3
  181.7 0.0 copy-start.5
  181.7 1.1 copy-done.5
  182.8 1.7 shard_map.76
Async XLA Ops:
  176.8 0.9 copy-start
  177.7 0.9 copy-start.2
  178.5 0.9 copy-start.4
  179.4 1.1 copy-start.1
  180.5 1.1 copy-start.3
  181.7 1.1 copy-start.5

commit v6 on v5

--- a/solution.py
+++ b/solution.py
@@ -196,7 +196,6 @@
                 p = mix_b(ps[k][lb, rows, :], 0, nxt, lb, k, b) - LEARN_RATE * y
                 ps[k][lb, rows, :] = p
                 sp[k][slot, lb, rows, :] = p.astype(BF16)
-                sy[k][nxt, lb, rows, :] = y.astype(BF16)
 
             @pl.when(t < steps)
             def _():
@@ -207,6 +206,8 @@
             def _():
                 p_st[k][lb + 1, block(k, pos), :] = ps[k][lb, block(k, pos), :]
                 start(p_swap_f32(lb, (k,)))
+
+            sy[k][nxt, lb] = ys[k][lb].astype(BF16)
 
         @pl.when(t < steps)
         def _():

time: 185 us -> 185 us (level)
  no operation moved by 1% of the time
where the time goes in v6:
time: 185 us; the launch traced here: 184 us
  Pallas kernels  178 us (96%)
  local copies, waits for them, and re-layouts  6.03 us (3%)
    pallas_call x1, Pallas kernels, device_fn(): pl.pallas_call(functools.partial(kernel, (size_x, size_y, layers, steps))...  176 us
    unnamed x12, local copies, waits for them, and re-layouts  6.03 us

profile of v6, /device:TPU:0, one launch (start us, length us, event | category | flops | bytes accessed | tf_op | source)
XLA Modules:
  0.0 184.3 jit_solution(17161996329346167511)
XLA Ops:
  0.6 175.9 %shard_map.75 = (f32[3,128,512]{2,1,0:T(8,128)S(1)}, f32[3,512,128]{2,1,0:T(8,128)S(1)}, f32[3,128,512]{2,1,0:T(8,128)S(1)}, f32[3,512,128]{2,1,0:T(8,128)S(1)}) custom-call(f32[3,128,512]{2,1,0:T(8,128)} %bitcast.10, f32[3,512,128]{2,1,0:T(8,128)} %bitcast.11, bf16[7,2048,128]{2,1,0:T(8,128)(2,1)} %bitcast.8, bf16[7,2048,128]{2,1,0:T(8,128)(2,1)} %bitcast.9), custom_call_target="tpu_custom_call" | custom-call | tf_op jit(solution)/shard_map/pallas_call | solution.py:417
  176.6 0.0 copy-start
  176.6 0.9 copy-done
  177.4 0.0 copy-start.2
  177.4 0.9 copy-done.2
  178.3 0.0 copy-start.4
  178.3 0.9 copy-done.4
  179.2 0.0 copy-start.1
  179.2 1.1 copy-done.1
  180.3 0.0 copy-start.3
  180.3 1.1 copy-done.3
  181.5 0.0 copy-start.5
  181.5 1.1 copy-done.5
  182.6 1.7 shard_map.76
Async XLA Ops:
  176.6 0.9 copy-start
  177.4 0.9 copy-start.2
  178.3 0.9 copy-start.4
  179.2 1.1 copy-start.1
  180.3 1.1 copy-start.3
  181.5 1.1 copy-start.5
